TPU v7x, 32 devices: a whole 2x2x4 slice. The times are simulated.
32 devices in a mesh: col: 8 (over z, y), row: 4 (over x, core).
Axes of the slice: x: 2, y: 2, z: 4, core: 2. Of those that a mesh axis runs over, the one named last changes fastest.
Arguments:
- inter_mask: int32 [65536, 4096], P('row', 'col')
- emb_user: bfloat16 [65536, 64], P(('row', 'col'))
- emb_item: bfloat16 [4096, 64], P(('col', 'row'))
- triples: int32 [128, 3], replicated
Outputs:
- output 1: bfloat16 [65536, 64], P(('row', 'col'))
- output 2: bfloat16 [4096, 64], P(('col', 'row'))
- output 3: float32 [], replicated
All inputs are finite; a program needn't handle non-finite values.
Results may differ from a plain program's by a relative error of at most 0.00519882.
Values are sent between devices in bfloat16 or wider.
A program may use at most 1 GiB of HBM per device.

v0:
```python
import jax
import jax.numpy as jnp
from jax import lax
from jax.sharding import PartitionSpec as P, NamedSharding

LAYERS = 3


def lookup_rows(emb_table, row_ids, row_base):
    local_ids = row_ids - row_base
    inside = (local_ids >= 0) & (local_ids < emb_table.shape[0])
    got_rows = jnp.take(emb_table, jnp.clip(local_ids, 0, emb_table.shape[0] - 1), axis=0).astype(jnp.float32)
    return jnp.where(inside[:, None], got_rows, 0.0)


def solution(mesh):
    row_count = mesh.shape["row"]
    col_count = mesh.shape["col"]

    def local_prog(mask_blk, user_shard, item_shard, triples):
        row_idx = lax.axis_index("row")
        col_idx = lax.axis_index("col")
        deg_user = jnp.maximum(lax.psum(jnp.sum(mask_blk, axis=1), "col"), 1)
        deg_item = jnp.maximum(lax.psum(jnp.sum(mask_blk, axis=0), "row"), 1)
        scale_user = lax.rsqrt(deg_user.astype(jnp.float32))
        scale_item = lax.rsqrt(deg_item.astype(jnp.float32))
        norm_adj = (mask_blk.astype(jnp.float32) * scale_user[:, None] * scale_item[None, :]).astype(jnp.bfloat16)
        layer_user = user_shard
        layer_item = item_shard
        total_user = user_shard.astype(jnp.float32)
        total_item = item_shard.astype(jnp.float32)
        for layer_idx in range(LAYERS):
            item_panel = lax.all_gather(layer_item, "row", axis=0, tiled=True)
            user_part = jnp.dot(norm_adj, item_panel, preferred_element_type=jnp.float32)
            next_user = lax.psum_scatter(user_part, "col", scatter_dimension=0, tiled=True).astype(jnp.bfloat16)
            user_panel = lax.all_gather(layer_user, "col", axis=0, tiled=True)
            item_part = lax.dot_general(norm_adj, user_panel, (((0,), (0,)), ((), ())), preferred_element_type=jnp.float32)
            next_item = lax.psum_scatter(item_part, "row", scatter_dimension=0, tiled=True).astype(jnp.bfloat16)
            total_user = total_user + next_user.astype(jnp.float32)
            total_item = total_item + next_item.astype(jnp.float32)
            layer_user = next_user
            layer_item = next_item
        out_user = (total_user / (LAYERS + 1)).astype(jnp.bfloat16)
        out_item = (total_item / (LAYERS + 1)).astype(jnp.bfloat16)
        user_base = (row_idx * col_count + col_idx) * out_user.shape[0]
        item_base = (col_idx * row_count + row_idx) * out_item.shape[0]
        trip_count = triples.shape[0]
        picked = jnp.concatenate([lookup_rows(out_user, triples[:, 0], user_base), lookup_rows(out_item, triples[:, 1], item_base), lookup_rows(out_item, triples[:, 2], item_base)], axis=0)
        picked = lax.psum(picked, ("row", "col"))
        user_vec = picked[:trip_count]
        pos_vec = picked[trip_count:2 * trip_count]
        neg_vec = picked[2 * trip_count:]
        margin = jnp.sum(user_vec * pos_vec, axis=1) - jnp.sum(user_vec * neg_vec, axis=1)
        bpr_loss = jnp.mean(jax.nn.softplus(-margin))
        return out_user, out_item, bpr_loss

    return jax.shard_map(local_prog, mesh=mesh, in_specs=(P("row", "col"), P(("row", "col"), None), P(("col", "row"), None), P(None, None)), out_specs=(P(("row", "col"), None), P(("col", "row"), None), P()), check_vma=False)
```

profile of v0, /device:TPU:0, one launch (start us, length us, event | category | flops | bytes accessed | tf_op | source)
XLA Modules:
  0.0 750.9 jit_solution(17373626337584873997)
XLA Ops:
  7.2 12.9 %fusion.3 = (s32[16384]{0:T(1024)}, s32[512]{0:T(512)S(1)}) fusion(s32[16384,512]{1,0:T(8,128)} %param.6), kind=kLoop, calls=%fused_computation.33 | loop fusion | flops 16760320 | bytes 33622016 | tf_op jit(solution)/shard_map/reduce_sum | solution.py:23
  20.2 0.7 all-gather.4.cloned.1.call-update
  20.9 6.4 psum.22
  27.4 5.3 all_gather.18
  32.7 59.7 %all-reduce.3.cloned.1.call-done = s32[16384]{0:T(1024)} async-done(((s32[16384]{0:T(1024)}), s32[16384]{0:T(1024)}) %all-reduce.3.cloned.1.call-update) | async-done | bytes 65552 | tf_op jit(solution)/shard_map/psum | solution.py:23
  92.4 0.9 convert_rsqrt_fusion
  93.2 18.3 %multiply_convert_fusion = bf16[16384,512]{1,0:T(8,128)(2,1)} fusion(s32[16384,512]{1,0:T(8,128)} %param.6, f32[512]{0:T(512)S(1)} %convert_rsqrt_fusion.1, f32[16384]{0:T(1024)S(1)} %convert_rsqrt_fusion), kind=kLoop, calls=%fused_computation.3 | loop fusion | flops 33554432 | bytes 50399232 | tf_op jit(solution)/shard_map/convert_element_type | solution.py:27
  111.5 31.9 %all-gather.4.cloned.1.call-done = bf16[16384,64]{0,1:T(8,128)(2,1)} async-done(((bf16[2048,64]{0,1:T(8,128)(2,1)}), bf16[16384,64]{0,1:T(8,128)(2,1)}) %all-gather.4.cloned.1.call-update) | async-done | bytes 2097168 | tf_op jit(solution)/shard_map/all_gather | solution.py:36
  143.4 10.1 %fusion.7 = f32[512,64]{0,1:T(8,128)} fusion(bf16[16384,64]{0,1:T(8,128)(2,1)} %all-gather.4.cloned.1.call-done, bf16[16384,512]{1,0:T(8,128)(2,1)} %multiply_convert_fusion), kind=kOutput, calls=%fused_computation.37 | convolution fusion | flops 1073741824 | bytes 19005440 | tf_op jit(solution)/shard_map/dot_general | solution.py:37
  153.5 0.0 reduce-scatter.7.cloned.1.call-start
  153.6 12.9 %fusion.4 = f32[16384,64]{0,1:T(8,128)} fusion(bf16[16384,512]{1,0:T(8,128)(2,1)} %multiply_convert_fusion, bf16[512,64]{0,1:T(8,128)(2,1)S(1)} %all_gather.18), kind=kOutput, calls=%fused_computation.34 | convolution fusion | flops 1073741824 | bytes 21037056 | tf_op jit(solution)/shard_map/dot_general | solution.py:34
  166.5 0.0 reduce-scatter.11.cloned.1.call-start
  166.5 5.6 reduce-scatter.9.cloned.1.call-done
  172.1 0.8 convert_element_type.76
  172.9 5.3 all_gather.20
  178.2 12.8 %fusion.5 = f32[16384,64]{0,1:T(8,128)} fusion(bf16[16384,512]{1,0:T(8,128)(2,1)} %multiply_convert_fusion, bf16[512,64]{0,1:T(8,128)(2,1)S(1)} %all_gather.20), kind=kOutput, calls=%fused_computation.35 | convolution fusion | flops 1073741824 | bytes 21037056 | tf_op jit(solution)/shard_map/dot_general | solution.py:34
  191.0 0.0 all-gather.6.cloned.1.call-start
  191.1 73.0 %reduce-scatter.7.cloned.1.call-done = f32[2048,64]{0,1:T(8,128)} async-done(((f32[16384,64]{0,1:T(8,128)}), f32[2048,64]{0,1:T(8,128)}) %reduce-scatter.7.cloned.1.call-update) | async-done | bytes 524304 | tf_op jit(solution)/shard_map/reduce_scatter | solution.py:35
  264.1 1.8 convert_element_type.74
  265.9 0.0 all-gather.8.cloned.1.call-start
  265.9 89.6 %reduce-scatter.11.cloned.1.call-done = f32[2048,64]{0,1:T(8,128)} async-done(((f32[16384,64]{0,1:T(8,128)}), f32[2048,64]{0,1:T(8,128)}) %reduce-scatter.11.cloned.1.call-update) | async-done | bytes 524304 | tf_op jit(solution)/shard_map/reduce_scatter | solution.py:35
  355.5 1.8 convert_element_type.77
  357.3 0.0 reduce-scatter.13.cloned.1.call-start
  357.3 48.9 %all-gather.6.cloned.1.call-done = bf16[16384,64]{0,1:T(8,128)(2,1)} async-done(((bf16[2048,64]{0,1:T(8,128)(2,1)}), bf16[16384,64]{0,1:T(8,128)(2,1)}) %all-gather.6.cloned.1.call-update) | async-done | bytes 2097168 | tf_op jit(solution)/shard_map/all_gather | solution.py:36
  406.2 10.1 %fusion.8 = f32[512,64]{0,1:T(8,128)} fusion(bf16[16384,64]{0,1:T(8,128)(2,1)} %all-gather.6.cloned.1.call-done, bf16[16384,512]{1,0:T(8,128)(2,1)} %multiply_convert_fusion), kind=kOutput, calls=%fused_computation.38 | convolution fusion | flops 1073741824 | bytes 19005440 | tf_op jit(solution)/shard_map/dot_general | solution.py:37
  416.3 0.2 reduce-scatter.17.cloned.1.call-start
  416.5 40.5 %all-gather.8.cloned.1.call-done = bf16[16384,64]{0,1:T(8,128)(2,1)} async-done(((bf16[2048,64]{0,1:T(8,128)(2,1)}), bf16[16384,64]{0,1:T(8,128)(2,1)}) %all-gather.8.cloned.1.call-update) | async-done | bytes 2097168 | tf_op jit(solution)/shard_map/all_gather | solution.py:36
  457.1 10.1 %fusion.9 = f32[512,64]{0,1:T(8,128)} fusion(bf16[16384,64]{0,1:T(8,128)(2,1)} %all-gather.8.cloned.1.call-done, bf16[16384,512]{1,0:T(8,128)(2,1)} %multiply_convert_fusion), kind=kOutput, calls=%fused_computation.39 | convolution fusion | flops 1073741824 | bytes 19005440 | tf_op jit(solution)/shard_map/dot_general | solution.py:37
  467.2 0.0 reduce-scatter.15.cloned.1.call-start
  467.2 10.8 %reduce-scatter.13.cloned.1.call-done = f32[128,64]{0,1:T(8,128)} async-done(((f32[512,64]{0,1:T(8,128)}), f32[128,64]{0,1:T(8,128)}) %reduce-scatter.13.cloned.1.call-update) | async-done | bytes 32784 | tf_op jit(solution)/shard_map/reduce_scatter | solution.py:38
  478.0 22.7 %reduce-scatter.17.cloned.1.call-done = f32[128,64]{0,1:T(8,128)} async-done(((f32[512,64]{0,1:T(8,128)}), f32[128,64]{0,1:T(8,128)}) %reduce-scatter.17.cloned.1.call-update) | async-done | bytes 32784 | tf_op jit(solution)/shard_map/reduce_scatter | solution.py:38
  500.7 0.8 multiply_convert_fusion.2
  501.5 5.3 all_gather.22
  506.8 12.8 %fusion.6 = f32[16384,64]{0,1:T(8,128)} fusion(bf16[16384,512]{1,0:T(8,128)(2,1)} %multiply_convert_fusion, bf16[512,64]{0,1:T(8,128)(2,1)S(1)} %all_gather.22), kind=kOutput, calls=%fused_computation.36 | convolution fusion | flops 1073741824 | bytes 21037056 | tf_op jit(solution)/shard_map/dot_general | solution.py:34
  519.6 0.0 all-reduce.5.cloned.1.call-start
  519.7 0.1 copy.8
  519.9 0.7 gather_fusion.1
  520.6 0.7 gather_fusion.2
  521.3 0.1 convert_select_fusion
  521.4 86.8 %reduce-scatter.15.cloned.1.call-done = f32[2048,64]{0,1:T(8,128)} async-done(((f32[16384,64]{0,1:T(8,128)}), f32[2048,64]{0,1:T(8,128)}) %reduce-scatter.15.cloned.1.call-update) | async-done | bytes 524304 | tf_op jit(solution)/shard_map/reduce_scatter | solution.py:35
  608.2 1.1 multiply_convert_fusion.1
  609.4 0.3 copy.7
  609.7 0.7 gather_fusion
  610.4 0.1 convert_select_fusion.2
  610.5 0.7 pad_maximum_fusion
  611.2 129.7 %all-reduce.5.cloned.1.call-done = f32[384,64]{1,0:T(8,128)} async-done(((f32[384,64]{1,0:T(8,128)}), f32[384,64]{1,0:T(8,128)}) %all-reduce.5.cloned.1.call-update) | async-done | bytes 98320 | tf_op jit(solution)/shard_map/psum | solution.py:49
  740.9 1.0 fusion
  741.9 0.6 fusion.2
  (35 shorter events, 0.4 us)
Async XLA Ops:
  7.2 20.2 %copy-start.5 = (bf16[128,64]{0,1:T(8,128)(2,1)S(1)}, bf16[128,64]{0,1:T(8,128)(2,1)}, u32[]{:S(2)}) copy-start(bf16[128,64]{0,1:T(8,128)(2,1)} %param.8) | copy-start | bytes 49156
  7.2 85.2 %all-reduce.3.cloned.1.call-start = ((), (), s32[]{:S(2)}) async-start(), calls=%async_computation.6 | async-start | bytes 131072 | tf_op jit(solution)/shard_map/psum | solution.py:23
  20.1 123.3 %all-gather.4.cloned.1.call-start = ((), (), s32[]{:S(2)}) async-start(), calls=%async_computation.8 | async-start | bytes 2359296 | tf_op jit(solution)/shard_map/all_gather | solution.py:36
  20.9 151.3 %reduce-scatter.9.cloned.1.call-start = ((), (), s32[]{:S(2)}) async-start(), calls=%async_computation.9 | async-start | bytes 163840 | tf_op jit(solution)/shard_map/reduce_scatter | solution.py:38
  153.5 110.6 %reduce-scatter.7.cloned.1.call-start = ((), (), s32[]{:S(2)}) async-start(), calls=%async_computation.7 | async-start | bytes 4718592 | tf_op jit(solution)/shard_map/reduce_scatter | solution.py:35
  166.5 189.0 %reduce-scatter.11.cloned.1.call-start = ((), (), s32[]{:S(2)}) async-start(), calls=%async_computation.10 | async-start | bytes 4718592 | tf_op jit(solution)/shard_map/reduce_scatter | solution.py:35
  191.0 215.2 %all-gather.6.cloned.1.call-start = ((), (), s32[]{:S(2)}) async-start(), calls=%async_computation.11 | async-start | bytes 2359296 | tf_op jit(solution)/shard_map/all_gather | solution.py:36
  265.9 191.2 %all-gather.8.cloned.1.call-start = ((), (), s32[]{:S(2)}) async-start(), calls=%async_computation.14 | async-start | bytes 2359296 | tf_op jit(solution)/shard_map/all_gather | solution.py:36
  357.3 120.7 %reduce-scatter.13.cloned.1.call-start = ((), (), s32[]{:S(2)}) async-start(), calls=%async_computation.12 | async-start | bytes 163840 | tf_op jit(solution)/shard_map/reduce_scatter | solution.py:38
  416.3 84.4 %copy-start.4 = (f32[128,64]{0,1:T(8,128)S(1)}, f32[128,64]{0,1:T(8,128)}, u32[]{:S(2)}) copy-start(f32[128,64]{0,1:T(8,128)} %reduce-scatter.9.cloned.1.call-done) | copy-start | bytes 98308
  416.3 84.3 %reduce-scatter.17.cloned.1.call-start = ((), (), s32[]{:S(2)}) async-start(), calls=%async_computation.15 | async-start | bytes 163840 | tf_op jit(solution)/shard_map/reduce_scatter | solution.py:38
  467.1 52.5 %copy-start.7 = (s32[128,3]{0,1:T(4,128)S(1)}, s32[128,3]{0,1:T(4,128)}, u32[]{:S(2)}) copy-start(s32[128,3]{0,1:T(4,128)} %param.9) | copy-start | bytes 4612
  467.1 141.1 %copy-start = (f32[2048,64]{0,1:T(8,128)S(1)}, f32[2048,64]{0,1:T(8,128)}, u32[]{:S(2)}) copy-start(f32[2048,64]{0,1:T(8,128)} %reduce-scatter.7.cloned.1.call-done) | copy-start | bytes 1572868
  467.1 141.1 %copy-start.1 = (f32[2048,64]{0,1:T(8,128)S(1)}, f32[2048,64]{0,1:T(8,128)}, u32[]{:S(2)}) copy-start(f32[2048,64]{0,1:T(8,128)} %reduce-scatter.11.cloned.1.call-done) | copy-start | bytes 1572868
  467.1 141.1 %copy-start.3 = (bf16[2048,64]{0,1:T(8,128)(2,1)S(1)}, bf16[2048,64]{0,1:T(8,128)(2,1)}, u32[]{:S(2)}) copy-start(bf16[2048,64]{0,1:T(8,128)(2,1)} %param.7) | copy-start | bytes 786436
  467.2 141.0 %reduce-scatter.15.cloned.1.call-start = ((), (), s32[]{:S(2)}) async-start(), calls=%async_computation.13 | async-start | bytes 4718592 | tf_op jit(solution)/shard_map/reduce_scatter | solution.py:35
  501.4 241.7 %copy-start.6 = (bf16[128,64]{0,1:T(8,128)(2,1)}, bf16[128,64]{0,1:T(8,128)(2,1)S(1)}, u32[]{:S(2)}) copy-start(bf16[128,64]{0,1:T(8,128)(2,1)S(1)} %get-tuple-element.14) | copy-start | bytes 49156
  519.6 221.3 %all-reduce.5.cloned.1.call-start = ((), (), s32[]{:S(2)}) async-start(), calls=%async_computation.16 | async-start | bytes 393216 | tf_op jit(solution)/shard_map/psum | solution.py:49
  609.4 133.8 %copy-start.2 = (bf16[2048,64]{0,1:T(8,128)(2,1)}, bf16[2048,64]{0,1:T(8,128)(2,1)S(1)}, u32[]{:S(2)}) copy-start(bf16[2048,64]{0,1:T(8,128)(2,1)S(1)} %multiply_convert_fusion.1) | copy-start | bytes 786436
Sparse Core Ops, SparseCore 0:
  20.2 72.0 all-reduce.2
  94.6 48.8 all-gather.3
  153.6 18.4 reduce-scatter.8
  175.6 88.4 reduce-scatter.6
  267.6 87.8 reduce-scatter.10
  357.5 48.6 all-gather.5
  409.0 48.0 all-gather.7
  459.5 18.4 reduce-scatter.12
  481.0 19.6 reduce-scatter.16
  519.7 88.4 reduce-scatter.14
  613.8 127.0 all-reduce.4
where the time goes:
time: 752 us; the launch traced here: 751 us
  waiting for transfers between devices  600 us (80%)
  matrix products  68.7 us (9%)
  other arithmetic  40.8 us (5%)
  blocking collectives  22.3 us (3%)
  between operations  15.8 us (2%)
    reduce_scatter x3, waiting for transfers between devices, local_prog(): lax.psum_scatter(user_part, 'col', scatter_dimension=0, tiled=True)  249 us
    psum x1, waiting for transfers between devices, local_prog(): picked = lax.psum(picked, ('row', 'col'))  130 us
    all_gather x3, waiting for transfers between devices, local_prog(): user_panel = lax.all_gather(layer_user, 'col', axis=0, tiled=True)  121 us
    psum x1, waiting for transfers between devices, local_prog(): deg_user = jnp.maximum(lax.psum(jnp.sum(mask_blk, axis=1), 'col'), 1)  59.7 us
    reduce_scatter x3, waiting for transfers between devices, local_prog(): lax.psum_scatter(item_part, 'row', scatter_dimension=0, tiled=True)  39.1 us
    dot_general x3, matrix products, local_prog(): jnp.dot(norm_adj, item_panel, preferred_element_type=jnp.float32)  38.5 us
    dot_general x3, matrix products, local_prog(): lax.dot_general(norm_adj, user_panel, (((0,), (0,)), ((), ())), preferred...  30.2 us
    convert_element_type x1, other arithmetic, local_prog(): (mask_blk.astype(jnp.float32) * scale_user[:, None] * scale_item[None, :]...  18.3 us
  transfers between devices with their start and end apart: 11, of which 11 were waited for; matrix products, arithmetic and copies ran while one was open for 9% of the time, Pallas kernels for 0%

commit v1 on v0

v1 whole, which is shorter than its diff:
```python
import functools

import jax
import jax.numpy as jnp
from jax import lax
from jax.experimental import pallas as pl
from jax.experimental.pallas import tpu as pltpu
from jax.sharding import PartitionSpec as P

LAYERS = 3
RING = 8
ROWS = 4
STREAMS = 4
DIM = 64
BLK = 512
MASK_BUFS = 8
MESH = pl.DeviceIdType.MESH
BF16 = jnp.bfloat16
F32 = jnp.float32
ORDER = (0, 2, 1, 3)


def sign(j):
    return 1 if j < 2 else -1


def col_of(p):
    p = lax.rem(p + 2 * RING, RING)
    y = lax.div(p, 4)
    z = p + y * (7 - 2 * p)
    return 2 * z + y


def dot_t(lhs, rhs):
    return lax.dot_general(lhs, rhs, (((1,), (1,)), ((), ())), preferred_element_type=F32)


def dot_n(lhs, rhs):
    return lax.dot_general(lhs, rhs, (((1,), (0,)), ((), ())), preferred_element_type=F32)


def kernel(mask_hbm, euT, eiT, trip, outu, outi, loss,
           adj, mbuf, msem,
           panel0, panel1, panel2, ei_all, item_acc, item_send, item_recv,
           slots, first,
           colsum, deg_part, deg_recv, scale_u, itemdeg, itemdeg_recv, scale_v,
           onehot_a, pk, pk_recv, picks, terms, terms2,
           ag_ss, ag_rs, rs_ss, rs_rs,
           row_ss, row_rs, col_ss, col_rs):
    c = lax.axis_index("col")
    r = lax.axis_index("row")
    z, y = lax.div(c, 2), lax.rem(c, 2)
    pos = z + y * (7 - 2 * z)
    right, left = col_of(pos + 1), col_of(pos - 1)
    row_peers = [lax.rem(r + d, ROWS) for d in range(1, ROWS)]
    col_peers = [lax.rem(c + d, RING) for d in range(1, RING)]
    panels = (panel0, panel1, panel2)

    def mask_copy(i):
        slot = lax.rem(i, MASK_BUFS)
        return pltpu.make_async_copy(mask_hbm.at[pl.ds(i * BLK, BLK), :], mbuf.at[slot], msem.at[slot])

    for i in range(MASK_BUFS):
        mask_copy(i).start()

    barrier = pltpu.get_barrier_semaphore()
    for rr in row_peers:
        pl.semaphore_signal(barrier, inc=1, device_id=(c, rr), device_id_type=MESH)
    for cc in col_peers:
        pl.semaphore_signal(barrier, inc=1, device_id=(cc, r), device_id_type=MESH)

    for j in range(STREAMS):
        panel0[c, j] = euT[:, j * BLK:(j + 1) * BLK]
    ei_all[0, r] = eiT[...]
    colsum[...] = jnp.zeros_like(colsum)
    pl.semaphore_wait(barrier, (ROWS - 1) + (RING - 1))

    def ring_dev(j):
        return (right if sign(j) > 0 else left, r)

    def ag_copy(k, j, s):
        q = col_of(pos - sign(j) * s)
        ref = panels[k].at[q, j]
        return pltpu.make_async_remote_copy(src_ref=ref, dst_ref=ref, send_sem=ag_ss.at[k, j, s],
                                            recv_sem=ag_rs.at[k, j, s], device_id=ring_dev(j), device_id_type=MESH)

    def ag_step(k, j, s, last=False):
        ag_copy(k, j, s).wait_recv()
        if not last:
            ag_copy(k, j, s + 1).start()

    def rs_copy(k, j, s, src=None):
        src = slots.at[k, j, s] if src is None else src
        return pltpu.make_async_remote_copy(src_ref=src, dst_ref=slots.at[k, j, s], send_sem=rs_ss.at[k, j, s],
                                            recv_sem=rs_rs.at[k, j, s], device_id=ring_dev(j), device_id_type=MESH)

    def row_send(u, src, dst):
        for rr in row_peers:
            pltpu.make_async_remote_copy(src_ref=src(rr), dst_ref=dst, send_sem=row_ss.at[u, rr],
                                         recv_sem=row_rs.at[u, r], device_id=(c, rr), device_id_type=MESH).start()

    def row_wait(u, src, dst):
        for rr in row_peers:
            cp = pltpu.make_async_remote_copy(src_ref=src(rr), dst_ref=dst(rr), send_sem=row_ss.at[u, rr],
                                              recv_sem=row_rs.at[u, rr], device_id=(c, rr), device_id_type=MESH)
            cp.wait_recv()
            cp.wait_send()

    def col_send(u, src, dst):
        for cc in col_peers:
            pltpu.make_async_remote_copy(src_ref=src(cc), dst_ref=dst, send_sem=col_ss.at[u, cc],
                                         recv_sem=col_rs.at[u, c], device_id=(cc, r), device_id_type=MESH).start()

    def col_wait(u, src, dst):
        for cc in col_peers:
            cp = pltpu.make_async_remote_copy(src_ref=src(cc), dst_ref=dst(cc), send_sem=col_ss.at[u, cc],
                                              recv_sem=col_rs.at[u, cc], device_id=(cc, r), device_id_type=MESH)
            cp.wait_recv()
            cp.wait_send()

    for j in ORDER:
        ag_copy(0, j, 0).start()
    row_send(0, lambda rr: ei_all.at[0, r], ei_all.at[0, r])

    ones = jnp.ones((16, BLK), BF16)

    def mask_block(i, carry):
        slot = lax.rem(i, MASK_BUFS)
        mask_copy(i).wait()
        acc = jnp.zeros((8, BLK), F32)
        for t in range(4):
            m = mbuf[slot, t * 128:(t + 1) * 128, :].astype(F32)
            acc = acc + jnp.sum(m.reshape(16, 8, BLK), axis=0)
            adj[i, t * 128:(t + 1) * 128, :] = m.astype(BF16)
        colsum[...] += acc
        deg_part[i] = dot_t(ones, adj[i])[0:1, :]

        @pl.when(i + MASK_BUFS < 4 * RING)
        def _():
            mask_copy(i + MASK_BUFS).start()
        return carry

    for s in range(4):
        lax.fori_loop(8 * s, 8 * s + 8, mask_block, 0)
        if s < 3:
            for j in ORDER:
                ag_step(0, j, s)

    shard = lambda ref, cc: ref.at[pl.ds(cc * STREAMS, STREAMS)]
    itemdeg[...] = jnp.sum(colsum[...], axis=0, keepdims=True)
    col_send(0, lambda cc: shard(deg_part, cc), deg_recv.at[c])
    row_send(1, lambda rr: itemdeg, itemdeg_recv.at[r])
    itemdeg_recv[r] = itemdeg[...]
    deg_recv[c] = deg_part[pl.ds(c * STREAMS, STREAMS)]
    for j in ORDER:
        ag_step(0, j, 3)
    row_wait(1, lambda rr: itemdeg, lambda rr: itemdeg_recv.at[rr])
    dv = itemdeg_recv[0] + itemdeg_recv[1] + itemdeg_recv[2] + itemdeg_recv[3]
    scale_v[...] = lax.rsqrt(jnp.maximum(dv, 1.0))
    col_wait(0, lambda cc: shard(deg_part, cc), lambda cc: deg_recv.at[cc])
    du = deg_recv[0]
    for q in range(1, RING):
        du = du + deg_recv[q]
    scale_u[pl.ds(c * STREAMS, STREAMS)] = lax.rsqrt(jnp.maximum(du, 1.0))
    col_send(1, lambda cc: shard(scale_u, c), shard(scale_u, c))
    for s in range(4, 7):
        for j in ORDER:
            ag_step(0, j, s, last=s == 6)
    row_wait(0, lambda rr: ei_all.at[0, r], lambda rr: ei_all.at[0, rr])
    col_wait(1, lambda cc: shard(scale_u, c), lambda cc: shard(scale_u, cc))

    def build(b):
        sv = scale_v[...]
        for t in range(4):
            su = scale_u[b, :, t * 128:(t + 1) * 128]
            suc = jnp.transpose(jnp.broadcast_to(su, (128, 128)))
            val = (jnp.concatenate([suc] * 4, axis=1) * sv).astype(BF16)
            adj[b, t * 128:(t + 1) * 128, :] = adj[b, t * 128:(t + 1) * 128, :] * val

    def block(j, off):
        return col_of(pos - sign(j) * off) * STREAMS + j

    def user_part(k, b):
        ei = jnp.concatenate([ei_all[k, q] for q in range(ROWS)], axis=1)
        return dot_t(ei, adj[b])

    def item_part(k, j, off):
        q = col_of(pos - sign(j) * off)
        item_acc[...] += dot_n(panels[k][q, j], adj[q * STREAMS + j])

    def item_start(k):
        for q in range(ROWS):
            item_send[k, q] = item_acc[:, q * 128:(q + 1) * 128]
        row_send(2 + 2 * k, lambda rr: item_send.at[k, rr], item_recv.at[k, r])
        item_recv[k, r] = item_send[k, r]
        item_acc[...] = jnp.zeros_like(item_acc)

    def item_sum(k):
        row_wait(2 + 2 * k, lambda rr: item_send.at[k, rr], lambda rr: item_recv.at[k, rr])
        tot = item_recv[k, 0] + item_recv[k, 1] + item_recv[k, 2] + item_recv[k, 3]
        return tot.astype(BF16)

    def item_share(k, val):
        ei_all[k + 1, r] = val
        row_send(3 + 2 * k, lambda rr: ei_all.at[k + 1, r], ei_all.at[k + 1, r])

    def item_end(k):
        row_wait(3 + 2 * k, lambda rr: ei_all.at[k + 1, r], lambda rr: ei_all.at[k + 1, rr])

    def rs_begin(k, make):
        for j in ORDER:
            b = block(j, 1)
            if make:
                build(b)
            first[k, j] = user_part(k, b)
            rs_copy(k, j, 0, first.at[k, j]).start()

    def rs_loop(k, lo, hi, make):
        def step(s, carry):
            for j in ORDER:
                b = block(j, s + 2)
                if make:
                    build(b)
                part = user_part(k, b)
                rs_copy(k, j, s).wait_recv()
                slots[k, j, s] = slots[k, j, s] + part
                pltpu.make_async_remote_copy(
                    src_ref=slots.at[k, j, s], dst_ref=slots.at[k, j, s + 1], send_sem=rs_ss.at[k, j, s + 1],
                    recv_sem=rs_rs.at[k, j, s + 1], device_id=ring_dev(j), device_id_type=MESH).start()
            if make:
                for j in ORDER:
                    item_part(0, j, s + 1)
            return carry
        lax.fori_loop(lo, hi, step, 0)

    def rs_end(k, make, then):
        for j in ORDER:
            b = block(j, 8)
            if make:
                build(b)
            part = user_part(k, b)
            rs_copy(k, j, 6).wait_recv()
            then(j, (slots[k, j, 6] + part).astype(BF16))

    def ag_loop(k, lo, hi):
        def step(s, carry):
            for j in ORDER:
                ag_step(k, j, s)
            for j in ORDER:
                item_part(k, j, s + 1)
            return carry
        lax.fori_loop(lo, hi, step, 0)

    def ag_begin(k):
        def then(j, val):
            panels[k][c, j] = val
            ag_copy(k, j, 0).start()
        return then

    def ag_end(k):
        for j in ORDER:
            ag_step(k, j, 6, last=True)
        for j in ORDER:
            item_part(k, j, 7)

    item_acc[...] = jnp.zeros_like(item_acc)
    rs_begin(0, True)
    rs_loop(0, 0, 6, True)
    rs_end(0, True, ag_begin(1))
    for off in (7, 8):
        for j in ORDER:
            item_part(0, j, off)
    item_start(0)
    for j in ORDER:
        item_part(1, j, 0)
    ag_loop(1, 0, 2)
    item_share(0, item_sum(0))
    ag_loop(1, 2, 6)
    ag_end(1)
    item_start(1)
    item_end(0)
    rs_begin(1, False)
    rs_loop(1, 0, 2, False)
    item_share(1, item_sum(1))
    rs_loop(1, 2, 6, False)
    rs_end(1, False, ag_begin(2))
    for j in ORDER:
        item_part(2, j, 0)
    ag_loop(2, 0, 6)
    ag_end(2)
    item_start(2)
    item_end(1)
    rs_begin(2, False)
    rs_loop(2, 0, 2, False)
    last_item = item_sum(2)
    tot = ei_all[0, r].astype(F32) + ei_all[1, r].astype(F32) + ei_all[2, r].astype(F32) + last_item.astype(F32)
    out_item = (tot / (LAYERS + 1)).astype(BF16)
    outi[...] = out_item
    item_share(2, out_item)
    rs_loop(2, 2, 3, False)
    item_end(2)
    iota_i = lax.broadcasted_iota(jnp.int32, (BLK, 128), 0) + c * BLK
    hot = jnp.concatenate([(iota_i == trip[1:2, :]).astype(BF16), (iota_i == trip[2:3, :]).astype(BF16)], axis=1)
    block_items = jnp.concatenate([ei_all[3, q] for q in range(ROWS)], axis=1)
    got = dot_n(block_items, hot).astype(BF16)
    for q in range(ROWS):
        pk[q] = got[q * 16:(q + 1) * 16, :]
    col_send(2, lambda cc: pk.at[r], pk_recv.at[c])
    pk_recv[c] = pk[r]
    rs_loop(2, 3, 5, False)
    col_wait(2, lambda cc: pk.at[r], lambda cc: pk_recv.at[cc])
    psum = pk_recv[0].astype(F32)
    for q in range(1, RING):
        psum = psum + pk_recv[q].astype(F32)
    picks[r] = psum.astype(BF16)
    row_send(8, lambda rr: picks.at[r], picks.at[r])
    base = (r * RING + c) * (STREAMS * BLK)
    ids_a = trip[0:1, :] - base
    for j in range(STREAMS):
        iota_u = lax.broadcasted_iota(jnp.int32, (BLK, 128), 0) + j * BLK
        onehot_a[j] = (iota_u == ids_a).astype(BF16)
    rs_loop(2, 5, 6, False)
    row_wait(8, lambda rr: picks.at[r], lambda rr: picks.at[rr])
    user_vec = []

    def finish(j, val):
        tot = (panel0[c, j].astype(F32) + panel1[c, j].astype(F32) + panel2[c, j].astype(F32) + val.astype(F32))
        out = (tot / (LAYERS + 1)).astype(BF16)
        outu[:, j * BLK:(j + 1) * BLK] = out
        user_vec.append(dot_n(out, onehot_a[j]))

    rs_end(2, False, finish)
    ea = user_vec[0] + user_vec[1] + user_vec[2] + user_vec[3]
    both = jnp.concatenate([picks[q] for q in range(ROWS)], axis=0).astype(F32)
    margin = (jnp.sum(ea * both[:, 0:128], axis=0, keepdims=True)
              - jnp.sum(ea * both[:, 128:256], axis=0, keepdims=True))
    term = jnp.maximum(-margin, 0.0) + jnp.log1p(jnp.exp(-jnp.abs(margin)))
    mine = jnp.logical_and(ids_a >= 0, ids_a < STREAMS * BLK)
    terms[r] = jnp.where(mine, term, 0.0)
    row_send(9, lambda rr: terms.at[r], terms.at[r])
    row_wait(9, lambda rr: terms.at[r], lambda rr: terms.at[rr])
    terms2[c] = terms[0] + terms[1] + terms[2] + terms[3]
    col_send(3, lambda cc: terms2.at[c], terms2.at[c])
    col_wait(3, lambda cc: terms2.at[c], lambda cc: terms2.at[cc])
    tsum = terms2[0]
    for q in range(1, RING):
        tsum = tsum + terms2[q]
    loss[...] = jnp.broadcast_to(jnp.sum(tsum, axis=1, keepdims=True) / tsum.shape[1], loss.shape)

    def drain(s, carry):
        for k in range(LAYERS):
            for j in range(STREAMS):
                ag_copy(k, j, s).wait_send()
                rs_copy(k, j, s).wait_send()
        return carry
    lax.fori_loop(0, RING - 1, drain, 0)


def solution(mesh):
    def local_prog(mask_blk, user_shard, item_shard, triples):
        vmem = pl.BlockSpec(memory_space=pltpu.VMEM)
        dma = pltpu.SemaphoreType.DMA
        outu, outi, loss = pl.pallas_call(
            kernel,
            out_shape=(jax.ShapeDtypeStruct((DIM, STREAMS * BLK), BF16),
                       jax.ShapeDtypeStruct((DIM, 128), BF16),
                       jax.ShapeDtypeStruct((8, 128), F32)),
            in_specs=[pl.BlockSpec(memory_space=pl.ANY), vmem, vmem, vmem],
            out_specs=(vmem, vmem, vmem),
            scratch_shapes=[
                pltpu.VMEM((RING * STREAMS, BLK, BLK), BF16),
                pltpu.VMEM((MASK_BUFS, BLK, BLK), jnp.int32),
                dma((MASK_BUFS,)),
                pltpu.VMEM((RING, STREAMS, DIM, BLK), BF16),
                pltpu.VMEM((RING, STREAMS, DIM, BLK), BF16),
                pltpu.VMEM((RING, STREAMS, DIM, BLK), BF16),
                pltpu.VMEM((LAYERS + 1, ROWS, DIM, 128), BF16),
                pltpu.VMEM((DIM, BLK), F32),
                pltpu.VMEM((LAYERS, ROWS, DIM, 128), F32),
                pltpu.VMEM((LAYERS, ROWS, DIM, 128), F32),
                pltpu.VMEM((LAYERS, STREAMS, RING - 1, DIM, BLK), F32),
                pltpu.VMEM((LAYERS, STREAMS, DIM, BLK), F32),
                pltpu.VMEM((8, BLK), F32),
                pltpu.VMEM((RING * STREAMS, 1, BLK), F32),
                pltpu.VMEM((RING, STREAMS, 1, BLK), F32),
                pltpu.VMEM((RING * STREAMS, 1, BLK), F32),
                pltpu.VMEM((1, BLK), F32),
                pltpu.VMEM((ROWS, 1, BLK), F32),
                pltpu.VMEM((1, BLK), F32),
                pltpu.VMEM((STREAMS, BLK, 128), BF16),
                pltpu.VMEM((ROWS, 16, 256), BF16),
                pltpu.VMEM((RING, 16, 256), BF16),
                pltpu.VMEM((ROWS, 16, 256), BF16),
                pltpu.VMEM((ROWS, 1, 128), F32),
                pltpu.VMEM((RING, 1, 128), F32),
                dma((LAYERS, STREAMS, RING - 1)), dma((LAYERS, STREAMS, RING - 1)),
                dma((LAYERS, STREAMS, RING - 1)), dma((LAYERS, STREAMS, RING - 1)),
                dma((10, ROWS)), dma((10, ROWS)),
                dma((4, RING)), dma((4, RING)),
            ],
            compiler_params=pltpu.CompilerParams(
                collective_id=0, has_side_effects=True, vmem_limit_bytes=60 * 1024 * 1024),
            name="propagate",
        )(mask_blk, user_shard.T, item_shard.T, triples.T)
        return outu.T, outi.T, loss[0, 0]

    return jax.shard_map(local_prog, mesh=mesh,
                         in_specs=(P("row", "col"), P(("row", "col"), None), P(("col", "row"), None), P(None, None)),
                         out_specs=(P(("row", "col"), None), P(("col", "row"), None), P()), check_vma=False)
```

time: 752 us -> 228 us (0.30)
  waiting for transfers between devices: 600 us -> 0 us
  Pallas kernels: 0 us -> 223 us
  matrix products: 68.7 us -> 0 us
  other arithmetic: 40.8 us -> 0 us
  blocking collectives: 22.3 us -> 0 us
  between operations: 15.8 us -> 0.64 us
    reduce_scatter x6 -> x0, waiting for transfers between devices: 288 us -> none  [the longest x3 249 us: local_prog(): lax.psum_scatter(user_part, 'col', scatter_dimension=0, tiled=True)]
    pallas_call x0 -> x1, Pallas kernels: none -> 223 us  [local_prog(): pl.pallas_call(kernel, out_shape=(jax.ShapeDtypeStruct((DIM, STREAMS * BL...]
    psum x2 -> x0, waiting for transfers between devices: 189 us -> none  [the longest x1 130 us: local_prog(): picked = lax.psum(picked, ('row', 'col'))]
    all_gather x3 -> x0, waiting for transfers between devices: 121 us -> none  [local_prog(): user_panel = lax.all_gather(layer_user, 'col', axis=0, tiled=True)]
    dot_general x6 -> x0, matrix products: 68.7 us -> none  [the longest x3 38.5 us: local_prog(): jnp.dot(norm_adj, item_panel, preferred_element_type=jnp.float32)]
    convert_element_type x6 -> x0, other arithmetic: 24.5 us -> none  [the longest x1 18.3 us: local_prog(): (mask_blk.astype(jnp.float32) * scale_user[:, None] * scale_item[None, :]...]
    all_gather x3 -> x0, blocking collectives: 15.9 us -> none  [local_prog(): item_panel = lax.all_gather(layer_item, 'row', axis=0, tiled=True)]
    reduce_sum x3 -> x0, other arithmetic: 14.5 us -> none  [the longest x1 12.9 us: local_prog(): deg_user = jnp.maximum(lax.psum(jnp.sum(mask_blk, axis=1), 'col'), 1)]
  transfers between devices with their start and end apart: 11 -> 0, of which waited for: 11 -> 0; matrix products, arithmetic and copies ran while one was open for 9% -> 0% of each run, Pallas kernels for 0% -> 0%
where the time goes in v1:
time: 228 us
  Pallas kernels  223 us (98%)
  local copies, waits for them, and re-layouts  4.19 us (2%)
    pallas_call x1, Pallas kernels, local_prog(): pl.pallas_call(kernel, out_shape=(jax.ShapeDtypeStruct((DIM, STREAMS * BL...  223 us

profile of v1, /device:TPU:0, one launch (start us, length us, event | category | flops | bytes accessed | tf_op | source)
XLA Modules:
  0.0 227.9 jit_solution(7141484781148476678)
XLA Ops:
  0.6 223.1 %propagate.1 = (bf16[64,2048]{1,0:T(8,128)(2,1)}, bf16[64,128]{1,0:T(8,128)(2,1)}, f32[8,128]{1,0:T(8,128)}) custom-call(s32[16384,512]{1,0:T(8,128)} %mask_hbm.1, bf16[64,2048]{1,0:T(8,128)(2,1)} %bitcast.6, bf16[64,128]{1,0:T(8,128)(2,1)} %bitcast.8, s32[3,128]{1,0:T(4,128)} %bitcast.10), custom_call_target="tpu_custom_call" | custom-call | tf_op jit(solution)/shard_map/propagate/pallas_call | solution.py:363
  223.7 1.2 slice.3
  224.9 1.7 copy.9
  226.6 1.3 copy.10

commit v2 on v1

v2 whole, which is shorter than its diff:
```python
import jax
import jax.numpy as jnp
from jax import lax
from jax.experimental import pallas as pl
from jax.experimental.pallas import tpu as pltpu
from jax.sharding import PartitionSpec as P

LAYERS = 3
RING = 8
ROWS = 4
DEPTH = 4
ROUNDS = 16
AHEAD = 3
DELAY = 8
SUBS = 4
DIM = 64
BLK = 512
MASK_BUFS = 8
MESH = pl.DeviceIdType.MESH
BF16 = jnp.bfloat16
F32 = jnp.float32


def dot_t(lhs, rhs):
    return lax.dot_general(lhs, rhs, (((1,), (1,)), ((), ())), preferred_element_type=F32)


def dot_n(lhs, rhs):
    return lax.dot_general(lhs, rhs, (((1,), (0,)), ((), ())), preferred_element_type=F32)


def kernel(mask_hbm, euT, eiT, trip, outu, outi, loss,
           adj, mbuf, msem,
           panel0, panel1, panel2, ei_all, item_acc, item_send, item_recv,
           ysend, yrecv, zin,
           colsum, deg_part, deg_recv, scale_u, itemdeg, itemdeg_recv, scale_v,
           onehot_a, pk, pk_recv, picks, user_vec, terms, terms2,
           y_ss, y_rs, z_ss, z_rs, ag_sy, ag_s1, ag_s2, ag_rs,
           row_ss, row_rs, col_ss, col_rs):
    c = lax.axis_index("col")
    r = lax.axis_index("row")
    z, y = lax.div(c, 2), lax.rem(c, 2)
    mate = 2 * z + 1 - y
    is_up, is_down = z < DEPTH - 1, z > 0
    is_mid = jnp.logical_and(is_up, is_down)
    row_peers = [lax.rem(r + d, ROWS) for d in range(1, ROWS)]
    col_peers = [lax.rem(c + d, RING) for d in range(1, RING)]
    panels = (panel0, panel1, panel2)

    def mask_copy(i):
        slot = lax.rem(i, MASK_BUFS)
        return pltpu.make_async_copy(mask_hbm.at[pl.ds(i * BLK, BLK), :], mbuf.at[slot], msem.at[slot])

    for i in range(MASK_BUFS):
        mask_copy(i).start()

    barrier = pltpu.get_barrier_semaphore()
    for rr in row_peers:
        pl.semaphore_signal(barrier, inc=1, device_id=(c, rr), device_id_type=MESH)
    for cc in col_peers:
        pl.semaphore_signal(barrier, inc=1, device_id=(cc, r), device_id_type=MESH)

    def remote(src, dst, ss, rs, col):
        return pltpu.make_async_remote_copy(src_ref=src, dst_ref=dst, send_sem=ss, recv_sem=rs,
                                            device_id=(col, r), device_id_type=MESH)

    def ag_y(k, q, col):
        ref = panels[k].at[col, q]
        return remote(ref, ref, ag_sy.at[k, q], ag_rs.at[k, col, q], mate)

    def ag_up(k, col, q):
        ref = panels[k].at[col, q]
        return remote(ref, ref, ag_s1.at[k, col, q], ag_rs.at[k, col, q], c + 2)

    def ag_down(k, col, q):
        ref = panels[k].at[col, q]
        return remote(ref, ref, ag_s1.at[k, col, q], ag_rs.at[k, col, q], c - 2)

    def ag_down2(k, col, q):
        ref = panels[k].at[col, q]
        return remote(ref, ref, ag_s2.at[k, lax.rem(col, 2), q], ag_rs.at[k, col, q], c - 2)

    def ag_both(k, col, q):
        @pl.when(is_up)
        def _():
            ag_up(k, col, q).start()

        @pl.when(is_down)
        def _():
            ag_down2(k, col, q).start()

    def ag_own(k, q):
        ag_y(k, q, c).start()
        ag_both(k, c, q)

    def ag_mate(k, q):
        with jax.named_scope("ag%d_mate" % k):
            ag_y(k, q, mate).wait_recv()
        ag_both(k, mate, q)

    def ag_event(k, e, then):
        d, rest = lax.div(e, 2 * SUBS) + 1, lax.rem(e, 2 * SUBS)
        yy = y + lax.div(rest, SUBS) * (1 - 2 * y)
        q = lax.rem(rest, SUBS)

        @pl.when(z + d < DEPTH)
        def _():
            col = 2 * (z + d) + yy
            with jax.named_scope("ag%d_above" % k):
                ag_down(k, col, q).wait_recv()

            @pl.when(is_down)
            def _():
                ag_down(k, col, q).start()
            then(col, q)

        @pl.when(z - d >= 0)
        def _():
            col = 2 * (z - d) + yy
            with jax.named_scope("ag%d_below" % k):
                ag_up(k, col, q).wait_recv()

            @pl.when(is_up)
            def _():
                ag_up(k, col, q).start()
            then(col, q)

    def row_send(u, src, dst):
        for rr in row_peers:
            pltpu.make_async_remote_copy(src_ref=src(rr), dst_ref=dst, send_sem=row_ss.at[u, rr],
                                         recv_sem=row_rs.at[u, r], device_id=(c, rr), device_id_type=MESH).start()

    def row_wait(u, src, dst):
        with jax.named_scope("row_wait_%d" % u):
            for rr in row_peers:
                cp = pltpu.make_async_remote_copy(src_ref=src(rr), dst_ref=dst(rr), send_sem=row_ss.at[u, rr],
                                                  recv_sem=row_rs.at[u, rr], device_id=(c, rr), device_id_type=MESH)
                cp.wait_recv()
                cp.wait_send()

    def col_send(u, src, dst):
        for cc in col_peers:
            remote(src(cc), dst, col_ss.at[u, cc], col_rs.at[u, c], cc).start()

    def col_wait(u, src, dst):
        with jax.named_scope("col_wait_%d" % u):
            for cc in col_peers:
                cp = remote(src(cc), dst(cc), col_ss.at[u, cc], col_rs.at[u, cc], cc)
                cp.wait_recv()
                cp.wait_send()

    ones = jnp.ones((16, BLK), BF16)
    colsum[...] = jnp.zeros_like(colsum)

    def mask_block(i, carry):
        slot = lax.rem(i, MASK_BUFS)
        mask_copy(i).wait()
        acc = jnp.zeros((8, BLK), F32)
        for t in range(4):
            m = mbuf[slot, t * 128:(t + 1) * 128, :].astype(F32)
            acc = acc + jnp.sum(m.reshape(16, 8, BLK), axis=0)
            adj[i, t * 128:(t + 1) * 128, :] = m.astype(BF16)
        colsum[...] += acc
        deg_part[i] = dot_t(ones, adj[i])[0:1, :]

        @pl.when(i + MASK_BUFS < SUBS * RING)
        def _():
            mask_copy(i + MASK_BUFS).start()
        return carry

    with jax.named_scope("mask0"):
        lax.fori_loop(0, 8, mask_block, 0)
    for q in range(SUBS):
        panel0[c, q] = euT[:, q * BLK:(q + 1) * BLK]
    ei_all[0, r] = eiT[...]
    with jax.named_scope("entry"):
        pl.semaphore_wait(barrier, (ROWS - 1) + (RING - 1))
    for q in range(SUBS):
        ag_own(0, q)
    row_send(0, lambda rr: ei_all.at[0, r], ei_all.at[0, r])
    with jax.named_scope("mask1"):
        lax.fori_loop(8, SUBS * RING, mask_block, 0)

    nothing = lambda col, q: None
    shard = lambda ref, cc: ref.at[pl.ds(cc * SUBS, SUBS)]
    itemdeg[...] = jnp.sum(colsum[...], axis=0, keepdims=True)
    col_send(0, lambda cc: shard(deg_part, cc), deg_recv.at[c])
    row_send(1, lambda rr: itemdeg, itemdeg_recv.at[r])
    itemdeg_recv[r] = itemdeg[...]
    deg_recv[c] = deg_part[pl.ds(c * SUBS, SUBS)]
    for q in range(SUBS):
        ag_mate(0, q)
    row_wait(1, lambda rr: itemdeg, lambda rr: itemdeg_recv.at[rr])
    dv = itemdeg_recv[0] + itemdeg_recv[1] + itemdeg_recv[2] + itemdeg_recv[3]
    scale_v[...] = lax.rsqrt(jnp.maximum(dv, 1.0))
    col_wait(0, lambda cc: shard(deg_part, cc), lambda cc: deg_recv.at[cc])
    du = deg_recv[0]
    for q in range(1, RING):
        du = du + deg_recv[q]
    scale_u[pl.ds(c * SUBS, SUBS)] = lax.rsqrt(jnp.maximum(du, 1.0))
    col_send(1, lambda cc: shard(scale_u, c), shard(scale_u, c))

    def early(e, carry):
        ag_event(0, e, nothing)
        return carry
    lax.fori_loop(0, DELAY, early, 0)
    row_wait(0, lambda rr: ei_all.at[0, r], lambda rr: ei_all.at[0, rr])
    col_wait(1, lambda cc: shard(scale_u, c), lambda cc: shard(scale_u, cc))

    def build(b):
        sv = scale_v[...]
        for t in range(4):
            su = scale_u[b, :, t * 128:(t + 1) * 128]
            suc = jnp.transpose(jnp.broadcast_to(su, (128, 128)))
            val = (jnp.concatenate([suc] * 4, axis=1) * sv).astype(BF16)
            adj[b, t * 128:(t + 1) * 128, :] = adj[b, t * 128:(t + 1) * 128, :] * val

    def user_part(k, b):
        ei = jnp.concatenate([ei_all[k, q] for q in range(ROWS)], axis=1)
        return dot_t(ei, adj[b])

    def item_part(k, col, q):
        item_acc[...] += dot_n(panels[k][col, q], adj[col * SUBS + q])

    def item_start(k):
        for q in range(ROWS):
            item_send[k, q] = item_acc[:, q * 128:(q + 1) * 128]
        row_send(2 + 2 * k, lambda rr: item_send.at[k, rr], item_recv.at[k, r])
        item_recv[k, r] = item_send[k, r]
        item_acc[...] = jnp.zeros_like(item_acc)

    def item_sum(k):
        row_wait(2 + 2 * k, lambda rr: item_send.at[k, rr], lambda rr: item_recv.at[k, rr])
        tot = item_recv[k, 0] + item_recv[k, 1] + item_recv[k, 2] + item_recv[k, 3]
        return tot.astype(BF16)

    def item_share(k, val):
        ei_all[k + 1, r] = val
        row_send(3 + 2 * k, lambda rr: ei_all.at[k + 1, r], ei_all.at[k + 1, r])

    def item_end(k):
        row_wait(3 + 2 * k, lambda rr: ei_all.at[k + 1, r], lambda rr: ei_all.at[k + 1, rr])

    def round_z(i):
        g = lax.div(i, SUBS)
        pw = 1 + 3 * g + 9 * lax.div(g * (g - 1), 2) + 27 * lax.div(g * (g - 1) * (g - 2), 6)
        return lax.rem(lax.div(27 + 48 * z + 57 * lax.div(z, 2), pw), 4)

    def y_copy(k, i):
        t, q = round_z(i), lax.rem(i, SUBS)
        return remote(ysend.at[k, t, q], yrecv.at[k, t, q], y_ss.at[k, t, q], y_rs.at[k, t, q], mate)

    def y_begin(k, i):
        t, q = round_z(i), lax.rem(i, SUBS)
        ysend[k, t, q] = user_part(k, (2 * t + 1 - y) * SUBS + q)
        y_copy(k, i).start()

    def z_up(k, t, q):
        return remote(yrecv.at[k, t, q], zin.at[k, t, q], z_ss.at[k, t, q], z_rs.at[k, t, q], c + 2)

    def z_down(k, t, q):
        to = t + lax.div(2 - (z - 1 - t), 2) * (DEPTH - t)
        return remote(yrecv.at[k, t, q], zin.at[k, to, q], z_ss.at[k, t, q], z_rs.at[k, to, q], c - 2)

    def z_add(k, t, at, q):
        with jax.named_scope("rs%d_z" % k):
            remote(yrecv.at[k, t, q], zin.at[k, at, q], z_ss.at[k, t, q], z_rs.at[k, at, q], mate).wait_recv()
        yrecv[k, t, q] = yrecv[k, t, q] + zin[k, at, q]

    def rs_round(k, i, then):
        t, q = round_z(i), lax.rem(i, SUBS)
        part = user_part(k, (2 * t + y) * SUBS + q)
        with jax.named_scope("rs%d_y" % k):
            y_copy(k, i).wait_recv()
        yrecv[k, t, q] = yrecv[k, t, q] + part

        @pl.when(i < 3 * SUBS)
        def _():
            @pl.when(is_mid)
            def _():
                z_add(k, t, t, q)

            @pl.when(t > z)
            def _():
                z_up(k, t, q).start()

            @pl.when(t < z)
            def _():
                z_down(k, t, q).start()

        @pl.when(i >= 3 * SUBS)
        def _():
            @pl.when(is_down)
            def _():
                z_add(k, z, z, q)

            @pl.when(is_up)
            def _():
                z_add(k, z, DEPTH, q)
            then(q, yrecv[k, z, q].astype(BF16))

    def table_end(k):
        def then(q, val):
            panels[k + 1][c, q] = val
            ag_own(k + 1, q)
        return then

    def build_round(i):
        t, q = round_z(i), lax.rem(i, SUBS)
        build((2 * t + 1 - y) * SUBS + q)
        build((2 * t + y) * SUBS + q)

    item_acc[...] = jnp.zeros_like(item_acc)

    for i in range(2):
        build_round(i)
        y_begin(0, i)
    for i in range(2, AHEAD + 1):
        build_round(i)
        if i < AHEAD:
            y_begin(0, i)

    def round_1(i, carry):
        @pl.when(i + AHEAD < ROUNDS)
        def _():
            y_begin(0, i + AHEAD)
        rs_round(0, i, table_end(0))

        @pl.when(i < 6)
        def _():
            build_round(2 * i + AHEAD + 1)
            build_round(2 * i + AHEAD + 2)

        @pl.when(i < (6 * SUBS - DELAY) // 2)
        def _():
            ag_event(0, DELAY + 2 * i, nothing)
            ag_event(0, DELAY + 2 * i + 1, nothing)

        @pl.when(jnp.logical_and(i >= 8, i < 12))
        def _():
            for a in range(2):
                for q in range(SUBS):
                    item_part(0, 2 * (i - 8) + a, q)

        @pl.when(i == 11)
        def _():
            item_start(0)

        @pl.when(i == 12)
        def _():
            item_share(0, item_sum(0))

        @pl.when(i == 13)
        def _():
            item_end(0)

        @pl.when(i >= 13)
        def _():
            y_begin(1, i - 13)
        return carry
    lax.fori_loop(0, ROUNDS, round_1, 0)

    def gather_round(k, i):
        @pl.when(i < SUBS)
        def _():
            ag_mate(k, i)
            item_part(k, c, i)
            item_part(k, mate, i)

        @pl.when(jnp.logical_and(i >= 1, i < 13))
        def _():
            ag_event(k, 2 * i - 2, lambda col, q: item_part(k, col, q))
            ag_event(k, 2 * i - 1, lambda col, q: item_part(k, col, q))

        @pl.when(i == 12)
        def _():
            item_start(k)

    def round_2(i, carry):
        @pl.when(i + AHEAD < ROUNDS)
        def _():
            y_begin(1, i + AHEAD)
        rs_round(1, i, table_end(1))
        gather_round(1, i)

        @pl.when(i == 13)
        def _():
            item_share(1, item_sum(1))

        @pl.when(i == 14)
        def _():
            item_end(1)

        @pl.when(i >= 14)
        def _():
            y_begin(2, i - 14)
        return carry
    lax.fori_loop(0, ROUNDS, round_2, 0)
    for i in range(2, AHEAD):
        y_begin(2, i)

    base = (r * RING + c) * (SUBS * BLK)
    ids_a = trip[0:1, :] - base
    user_vec[...] = jnp.zeros_like(user_vec)

    def finish(q, val):
        tot = (panel0[c, q].astype(F32) + panel1[c, q].astype(F32) + panel2[c, q].astype(F32) + val.astype(F32))
        out = (tot / (LAYERS + 1)).astype(BF16)
        outu[q] = out
        user_vec[...] += dot_n(out, onehot_a[q])

    def round_3(i, carry):
        @pl.when(i + AHEAD < ROUNDS)
        def _():
            y_begin(2, i + AHEAD)

        @pl.when(i < SUBS)
        def _():
            iota_u = lax.broadcasted_iota(jnp.int32, (BLK, 128), 0) + i * BLK
            onehot_a[i] = (iota_u == ids_a).astype(BF16)
        rs_round(2, i, finish)
        gather_round(2, i)

        @pl.when(i == 13)
        def _():
            last_item = item_sum(2)
            tot = (ei_all[0, r].astype(F32) + ei_all[1, r].astype(F32) + ei_all[2, r].astype(F32)
                   + last_item.astype(F32))
            out_item = (tot / (LAYERS + 1)).astype(BF16)
            outi[...] = out_item
            item_share(2, out_item)

        @pl.when(i == 14)
        def _():
            item_end(2)
            iota_i = lax.broadcasted_iota(jnp.int32, (BLK, 128), 0) + c * BLK
            hot = jnp.concatenate([(iota_i == trip[1:2, :]).astype(BF16), (iota_i == trip[2:3, :]).astype(BF16)],
                                  axis=1)
            got = dot_n(jnp.concatenate([ei_all[3, q] for q in range(ROWS)], axis=1), hot).astype(BF16)
            for q in range(ROWS):
                pk[q] = got[q * 16:(q + 1) * 16, :]
            col_send(2, lambda cc: pk.at[r], pk_recv.at[c])
            pk_recv[c] = pk[r]
        return carry
    lax.fori_loop(0, ROUNDS, round_3, 0)

    col_wait(2, lambda cc: pk.at[r], lambda cc: pk_recv.at[cc])
    psum = pk_recv[0].astype(F32)
    for q in range(1, RING):
        psum = psum + pk_recv[q].astype(F32)
    picks[r] = psum.astype(BF16)
    row_send(8, lambda rr: picks.at[r], picks.at[r])
    row_wait(8, lambda rr: picks.at[r], lambda rr: picks.at[rr])
    ea = user_vec[...]
    both = jnp.concatenate([picks[q] for q in range(ROWS)], axis=0).astype(F32)
    margin = (jnp.sum(ea * both[:, 0:128], axis=0, keepdims=True)
              - jnp.sum(ea * both[:, 128:256], axis=0, keepdims=True))
    term = jnp.maximum(-margin, 0.0) + jnp.log1p(jnp.exp(-jnp.abs(margin)))
    mine = jnp.logical_and(ids_a >= 0, ids_a < SUBS * BLK)
    terms[r] = jnp.where(mine, term, 0.0)
    row_send(9, lambda rr: terms.at[r], terms.at[r])
    row_wait(9, lambda rr: terms.at[r], lambda rr: terms.at[rr])
    terms2[c] = terms[0] + terms[1] + terms[2] + terms[3]
    col_send(3, lambda cc: terms2.at[c], terms2.at[c])

    def drain(i, carry):
        for k in range(LAYERS):
            t, q = round_z(i), lax.rem(i, SUBS)
            y_copy(k, i).wait_send()

            @pl.when(i < 3 * SUBS)
            def _():
                z_up(k, t, q).wait_send()

            @pl.when(i < SUBS)
            def _():
                ag_y(k, i, c).wait_send()
                for col in (c, mate):
                    @pl.when(is_up)
                    def _():
                        ag_up(k, col, i).wait_send()

                    @pl.when(is_down)
                    def _():
                        ag_down2(k, col, i).wait_send()
        return carry
    lax.fori_loop(0, ROUNDS, drain, 0)

    def drain_lines(e, carry):
        d, rest = lax.div(e, 2 * SUBS) + 1, lax.rem(e, 2 * SUBS)
        yy, q = lax.div(rest, SUBS), lax.rem(rest, SUBS)
        for k in range(LAYERS):
            @pl.when(jnp.logical_and(z + d < DEPTH, is_down))
            def _():
                ag_down(k, 2 * (z + d) + yy, q).wait_send()

            @pl.when(jnp.logical_and(z - d >= 0, is_up))
            def _():
                ag_up(k, 2 * (z - d) + yy, q).wait_send()
        return carry
    lax.fori_loop(0, 6 * SUBS, drain_lines, 0)

    col_wait(3, lambda cc: terms2.at[c], lambda cc: terms2.at[cc])
    tsum = terms2[0]
    for q in range(1, RING):
        tsum = tsum + terms2[q]
    loss[...] = jnp.broadcast_to(jnp.sum(tsum, axis=1, keepdims=True) / tsum.shape[1], loss.shape)


def solution(mesh):
    def local_prog(mask_blk, user_shard, item_shard, triples):
        vmem = pl.BlockSpec(memory_space=pltpu.VMEM)
        dma = pltpu.SemaphoreType.DMA
        outu, outi, loss = pl.pallas_call(
            kernel,
            out_shape=(jax.ShapeDtypeStruct((SUBS, DIM, BLK), BF16),
                       jax.ShapeDtypeStruct((DIM, 128), BF16),
                       jax.ShapeDtypeStruct((8, 128), F32)),
            in_specs=[pl.BlockSpec(memory_space=pl.ANY), vmem, vmem, vmem],
            out_specs=(vmem, vmem, vmem),
            scratch_shapes=[
                pltpu.VMEM((RING * SUBS, BLK, BLK), BF16),
                pltpu.VMEM((MASK_BUFS, BLK, BLK), jnp.int32),
                dma((MASK_BUFS,)),
                pltpu.VMEM((RING, SUBS, DIM, BLK), BF16),
                pltpu.VMEM((RING, SUBS, DIM, BLK), BF16),
                pltpu.VMEM((RING, SUBS, DIM, BLK), BF16),
                pltpu.VMEM((LAYERS + 1, ROWS, DIM, 128), BF16),
                pltpu.VMEM((DIM, BLK), F32),
                pltpu.VMEM((LAYERS, ROWS, DIM, 128), F32),
                pltpu.VMEM((LAYERS, ROWS, DIM, 128), F32),
                pltpu.VMEM((LAYERS, DEPTH, SUBS, DIM, BLK), F32),
                pltpu.VMEM((LAYERS, DEPTH, SUBS, DIM, BLK), F32),
                pltpu.VMEM((LAYERS, DEPTH + 1, SUBS, DIM, BLK), F32),
                pltpu.VMEM((8, BLK), F32),
                pltpu.VMEM((RING * SUBS, 1, BLK), F32),
                pltpu.VMEM((RING, SUBS, 1, BLK), F32),
                pltpu.VMEM((RING * SUBS, 1, BLK), F32),
                pltpu.VMEM((1, BLK), F32),
                pltpu.VMEM((ROWS, 1, BLK), F32),
                pltpu.VMEM((1, BLK), F32),
                pltpu.VMEM((SUBS, BLK, 128), BF16),
                pltpu.VMEM((ROWS, 16, 256), BF16),
                pltpu.VMEM((RING, 16, 256), BF16),
                pltpu.VMEM((ROWS, 16, 256), BF16),
                pltpu.VMEM((DIM, 128), F32),
                pltpu.VMEM((ROWS, 1, 128), F32),
                pltpu.VMEM((RING, 1, 128), F32),
                dma((LAYERS, DEPTH, SUBS)), dma((LAYERS, DEPTH, SUBS)),
                dma((LAYERS, DEPTH, SUBS)), dma((LAYERS, DEPTH + 1, SUBS)),
                dma((LAYERS, SUBS)), dma((LAYERS, RING, SUBS)), dma((LAYERS, 2, SUBS)), dma((LAYERS, RING, SUBS)),
                dma((10, ROWS)), dma((10, ROWS)),
                dma((4, RING)), dma((4, RING)),
            ],
            compiler_params=pltpu.CompilerParams(
                collective_id=0, has_side_effects=True, vmem_limit_bytes=61 * 1024 * 1024),
            name="propagate",
        )(mask_blk, user_shard.T, item_shard.T, triples.T)
        out_user = jnp.concatenate([outu[q] for q in range(SUBS)], axis=1).T
        return out_user, outi.T, loss[0, 0]

    return jax.shard_map(local_prog, mesh=mesh,
                         in_specs=(P("row", "col"), P(("row", "col"), None), P(("col", "row"), None), P(None, None)),
                         out_specs=(P(("row", "col"), None), P(("col", "row"), None), P()), check_vma=False)
```

time: 228 us -> 216 us (0.947)
  Pallas kernels: 223 us -> 211 us
    pallas_call x1, Pallas kernels: 223 us -> 211 us  [local_prog(): pl.pallas_call(kernel, out_shape=(jax.ShapeDtypeStruct((SUBS, DIM, BLK),...]
where the time goes in v2:
time: 216 us
  Pallas kernels  211 us (98%)
  local copies, waits for them, and re-layouts  3.46 us (2%)
    pallas_call x1, Pallas kernels, local_prog(): pl.pallas_call(kernel, out_shape=(jax.ShapeDtypeStruct((SUBS, DIM, BLK),...  211 us

profile of v2, /device:TPU:0, one launch (start us, length us, event | category | flops | bytes accessed | tf_op | source)
XLA Modules:
  0.0 215.7 jit_solution(4015640497927241472)
XLA Ops:
  0.6 210.9 %propagate.1 = (bf16[4,64,512]{2,1,0:T(8,128)(2,1)}, bf16[64,128]{1,0:T(8,128)(2,1)}, f32[8,128]{1,0:T(8,128)}) custom-call(s32[16384,512]{1,0:T(8,128)} %mask_hbm.1, bf16[64,2048]{1,0:T(8,128)(2,1)} %bitcast.15, bf16[64,128]{1,0:T(8,128)(2,1)} %bitcast.16, s32[3,128]{1,0:T(4,128)} %bitcast.18), custom_call_target="tpu_custom_call" | custom-call | tf_op jit(solution)/shard_map/propagate/pallas_call | solution.py:514
  211.5 1.2 slice.19
  212.7 1.0 slice_bitcast_fusion.3
  213.6 0.7 maximum_bitcast_fusion
  214.4 1.3 copy.8

commit v3 on v2

v3 whole, which is shorter than its diff:
```python
import jax
import jax.numpy as jnp
from jax import lax
from jax.experimental import pallas as pl
from jax.experimental.pallas import tpu as pltpu
from jax.sharding import PartitionSpec as P

LAYERS = 3
RING = 8
ROWS = 4
DEPTH = 4
ROUNDS = 16
AHEAD = 2
SUBS = 4
DIM = 64
BLK = 512
MASK_BUFS = 8
MESH = pl.DeviceIdType.MESH
BF16 = jnp.bfloat16
F32 = jnp.float32


def dot_t(lhs, rhs):
    return lax.dot_general(lhs, rhs, (((1,), (1,)), ((), ())), preferred_element_type=F32)


def dot_n(lhs, rhs):
    return lax.dot_general(lhs, rhs, (((1,), (0,)), ((), ())), preferred_element_type=F32)


def kernel(mask_hbm, euT, eiT, trip, outu, outi, loss,
           adj, mbuf, msem,
           panels, ei_all, item_acc, item_send, item_recv,
           ysend, yrecv, zin,
           colsum, deg_part, deg_recv, scale_u, itemdeg, itemdeg_recv, scale_v,
           onehot_a, pk, pk_recv, picks, user_vec, terms, terms2,
           y_ss, y_rs, z_ss, z_rs, ag_sy, ag_s1, ag_s2, ag_rs,
           row_ss, row_rs, col_ss, col_rs):
    c = lax.axis_index("col")
    r = lax.axis_index("row")
    z, y = lax.div(c, 2), lax.rem(c, 2)
    mate = 2 * z + 1 - y
    is_up, is_down = z < DEPTH - 1, z > 0
    is_mid = jnp.logical_and(is_up, is_down)
    row_peers = [lax.rem(r + d, ROWS) for d in range(1, ROWS)]
    col_peers = [lax.rem(c + d, RING) for d in range(1, RING)]

    def mask_at(i):
        return lax.rem(i, RING) * SUBS + lax.div(i, RING)

    def mask_copy(i):
        slot = lax.rem(i, MASK_BUFS)
        return pltpu.make_async_copy(mask_hbm.at[pl.ds(mask_at(i) * BLK, BLK), :], mbuf.at[slot], msem.at[slot])

    for i in range(MASK_BUFS):
        mask_copy(jnp.int32(i)).start()

    barrier = pltpu.get_barrier_semaphore()
    for rr in row_peers:
        pl.semaphore_signal(barrier, inc=1, device_id=(c, rr), device_id_type=MESH)
    for cc in col_peers:
        pl.semaphore_signal(barrier, inc=1, device_id=(cc, r), device_id_type=MESH)

    def remote(src, dst, ss, rs, col):
        return pltpu.make_async_remote_copy(src_ref=src, dst_ref=dst, send_sem=ss, recv_sem=rs,
                                            device_id=(col, r), device_id_type=MESH)

    def ag_y(k, q, col):
        ref = panels.at[k, col, q]
        return remote(ref, ref, ag_sy.at[k, q], ag_rs.at[k, col, q], mate)

    def ag_up(k, col, q):
        ref = panels.at[k, col, q]
        return remote(ref, ref, ag_s1.at[k, col, q], ag_rs.at[k, col, q], c + 2)

    def ag_down(k, col, q):
        ref = panels.at[k, col, q]
        return remote(ref, ref, ag_s1.at[k, col, q], ag_rs.at[k, col, q], c - 2)

    def ag_down2(k, col, q):
        ref = panels.at[k, col, q]
        return remote(ref, ref, ag_s2.at[k, lax.rem(col, 2), q], ag_rs.at[k, col, q], c - 2)

    def ag_both(k, col, q):
        @pl.when(is_up)
        def _():
            ag_up(k, col, q).start()

        @pl.when(is_down)
        def _():
            ag_down2(k, col, q).start()

    def ag_own(k, q):
        ag_y(k, q, c).start()
        ag_both(k, c, q)

    def ag_mate(k, q):
        with jax.named_scope("ag_mate"):
            ag_y(k, q, mate).wait_recv()
        ag_both(k, mate, q)

    def line_event(k, s, yy, q, above, then):
        col = 2 * s + yy
        if above:
            with jax.named_scope("ag_above"):
                ag_down(k, col, q).wait_recv()

            @pl.when(is_down)
            def _():
                ag_down(k, col, q).start()
        else:
            with jax.named_scope("ag_below"):
                ag_up(k, col, q).wait_recv()

            @pl.when(is_up)
            def _():
                ag_up(k, col, q).start()
        then(col, q)

    def first_event(e, event):
        d, rest = lax.div(e, 2 * SUBS) + 1, lax.rem(e, 2 * SUBS)
        yy = y + lax.div(rest, SUBS) * (1 - 2 * y)
        q = lax.rem(rest, SUBS)

        @pl.when(z + d < DEPTH)
        def _():
            event(z + d, yy, q, True)

        @pl.when(z - d >= 0)
        def _():
            event(z - d, yy, q, False)

    def row_send(u, src, dst):
        for rr in row_peers:
            pltpu.make_async_remote_copy(src_ref=src(rr), dst_ref=dst, send_sem=row_ss.at[u, rr],
                                         recv_sem=row_rs.at[u, r], device_id=(c, rr), device_id_type=MESH).start()

    def row_wait(u, src, dst):
        with jax.named_scope("row_wait_%d" % u):
            for rr in row_peers:
                cp = pltpu.make_async_remote_copy(src_ref=src(rr), dst_ref=dst(rr), send_sem=row_ss.at[u, rr],
                                                  recv_sem=row_rs.at[u, rr], device_id=(c, rr), device_id_type=MESH)
                cp.wait_recv()
                cp.wait_send()

    def col_send(u, src, dst):
        for cc in col_peers:
            remote(src(cc), dst, col_ss.at[u, cc], col_rs.at[u, c], cc).start()

    def col_wait(u, src, dst):
        with jax.named_scope("col_wait_%d" % u):
            for cc in col_peers:
                cp = remote(src(cc), dst(cc), col_ss.at[u, cc], col_rs.at[u, cc], cc)
                cp.wait_recv()
                cp.wait_send()

    ones = jnp.ones((16, BLK), BF16)
    colsum[...] = jnp.zeros_like(colsum)

    def mask_block(i, carry):
        slot, b = lax.rem(i, MASK_BUFS), mask_at(i)
        mask_copy(i).wait()
        acc = jnp.zeros((8, BLK), F32)
        for t in range(4):
            m = mbuf[slot, t * 128:(t + 1) * 128, :].astype(F32)
            acc = acc + jnp.sum(m.reshape(16, 8, BLK), axis=0)
            adj[b, t * 128:(t + 1) * 128, :] = m.astype(BF16)
        colsum[...] += acc
        deg_part[b] = dot_t(ones, adj[b])[0:1, :]

        @pl.when(i + MASK_BUFS < SUBS * RING)
        def _():
            mask_copy(i + MASK_BUFS).start()
        return carry

    def deg_send(q):
        col_send(q, lambda cc: deg_part.at[cc * SUBS + q], deg_recv.at[c, q])
        deg_recv[c, q] = deg_part[c * SUBS + q]

    def deg_sum(q):
        col_wait(q, lambda cc: deg_part.at[cc * SUBS + q], lambda cc: deg_recv.at[cc, q])
        du = deg_recv[0, q]
        for cc in range(1, RING):
            du = du + deg_recv[cc, q]
        scale_u[c * SUBS + q] = lax.rsqrt(jnp.maximum(du, 1.0))
        col_send(SUBS + q, lambda cc: scale_u.at[c * SUBS + q], scale_u.at[c * SUBS + q])

    def deg_end(q):
        col_wait(SUBS + q, lambda cc: scale_u.at[c * SUBS + q], lambda cc: scale_u.at[cc * SUBS + q])

    def mask_quarter(q):
        with jax.named_scope("mask"):
            lax.fori_loop(RING * q, RING * (q + 1), mask_block, 0)

    mask_quarter(0)
    for q in range(SUBS):
        panels[0, c, q] = euT[:, q * BLK:(q + 1) * BLK]
    ei_all[0, r] = eiT[...]
    with jax.named_scope("entry"):
        pl.semaphore_wait(barrier, (ROWS - 1) + (RING - 1))
    deg_send(0)
    for q in range(SUBS):
        ag_own(0, q)
    row_send(0, lambda rr: ei_all.at[0, r], ei_all.at[0, r])
    mask_quarter(1)
    deg_send(1)
    mask_quarter(2)
    deg_send(2)
    deg_sum(0)
    mask_quarter(3)
    itemdeg[...] = jnp.sum(colsum[...], axis=0, keepdims=True)
    row_send(1, lambda rr: itemdeg, itemdeg_recv.at[r])
    deg_send(3)
    itemdeg_recv[r] = itemdeg[...]
    nothing = lambda col, q: None
    deg_sum(1)
    for q in range(SUBS):
        ag_mate(0, q)
    deg_sum(2)
    row_wait(1, lambda rr: itemdeg, lambda rr: itemdeg_recv.at[rr])
    dv = itemdeg_recv[0] + itemdeg_recv[1] + itemdeg_recv[2] + itemdeg_recv[3]
    scale_v[...] = lax.rsqrt(jnp.maximum(dv, 1.0))
    row_wait(0, lambda rr: ei_all.at[0, r], lambda rr: ei_all.at[0, rr])
    deg_end(0)

    def build(b):
        sv = scale_v[...]
        for t in range(4):
            su = scale_u[b, :, t * 128:(t + 1) * 128]
            suc = jnp.transpose(jnp.broadcast_to(su, (128, 128)))
            val = (jnp.concatenate([suc] * 4, axis=1) * sv).astype(BF16)
            adj[b, t * 128:(t + 1) * 128, :] = adj[b, t * 128:(t + 1) * 128, :] * val

    def user_part(k, b):
        ei = jnp.concatenate([ei_all[k, q] for q in range(ROWS)], axis=1)
        return dot_t(ei, adj[b])

    def item_part(k, col, q):
        item_acc[k] += dot_n(panels[k, col, q], adj[col * SUBS + q])

    def item_start(k):
        for q in range(ROWS):
            item_send[k, q] = item_acc[k, :, q * 128:(q + 1) * 128]
        row_send(2 + 2 * k, lambda rr: item_send.at[k, rr], item_recv.at[k, r])
        item_recv[k, r] = item_send[k, r]

    def item_sum(k):
        row_wait(2 + 2 * k, lambda rr: item_send.at[k, rr], lambda rr: item_recv.at[k, rr])
        tot = item_recv[k, 0] + item_recv[k, 1] + item_recv[k, 2] + item_recv[k, 3]
        return tot.astype(BF16)

    def item_share(k, val):
        ei_all[k + 1, r] = val
        row_send(3 + 2 * k, lambda rr: ei_all.at[k + 1, r], ei_all.at[k + 1, r])

    def item_end(k):
        row_wait(3 + 2 * k, lambda rr: ei_all.at[k + 1, r], lambda rr: ei_all.at[k + 1, rr])

    def place(n):
        k, q, g = lax.div(n, ROUNDS), lax.rem(lax.div(n, DEPTH), SUBS), lax.rem(n, DEPTH)
        pw = 1 + 3 * g + 9 * lax.div(g * (g - 1), 2) + 27 * lax.div(g * (g - 1) * (g - 2), 6)
        return k, lax.rem(lax.div(27 + 48 * z + 57 * lax.div(z, 2), pw), DEPTH), q

    def y_copy(n):
        k, t, q = place(n)
        return remote(ysend.at[k, t, q], yrecv.at[k, t, q], y_ss.at[k, t, q], y_rs.at[k, t, q], mate)

    def y_begin(n):
        k, t, q = place(n)
        ysend[k, t, q] = user_part(k, (2 * t + 1 - y) * SUBS + q)
        y_copy(n).start()

    def z_up(k, t, q):
        return remote(yrecv.at[k, t, q], zin.at[k, t, q], z_ss.at[k, t, q], z_rs.at[k, t, q], c + 2)

    def z_down(k, t, q):
        to = t + lax.div(2 - (z - 1 - t), 2) * (DEPTH - t)
        return remote(yrecv.at[k, t, q], zin.at[k, to, q], z_ss.at[k, t, q], z_rs.at[k, to, q], c - 2)

    def z_add(k, t, at, q):
        with jax.named_scope("rs_z"):
            remote(yrecv.at[k, t, q], zin.at[k, at, q], z_ss.at[k, t, q], z_rs.at[k, at, q], mate).wait_recv()
        yrecv[k, t, q] = yrecv[k, t, q] + zin[k, at, q]

    def z_send(k, t, q):
        @pl.when(t > z)
        def _():
            z_up(k, t, q).start()

        @pl.when(t < z)
        def _():
            z_down(k, t, q).start()

    def y_stage(n):
        k, t, q = place(n)
        part = user_part(k, (2 * t + y) * SUBS + q)
        with jax.named_scope("rs_y"):
            y_copy(n).wait_recv()
        yrecv[k, t, q] = yrecv[k, t, q] + part

        @pl.when(jnp.logical_and(jnp.logical_not(is_mid), t != z))
        def _():
            z_send(k, t, q)

    def mid_stage(n):
        k, t, q = place(n)

        @pl.when(t != z)
        def _():
            z_add(k, t, t, q)
            z_send(k, t, q)

    def own_stage(n):
        k, _, q = place(n)

        @pl.when(is_down)
        def _():
            z_add(k, z, z, q)

        @pl.when(is_up)
        def _():
            z_add(k, z, DEPTH, q)
        val = yrecv[k, z, q].astype(BF16)

        @pl.when(k < LAYERS - 1)
        def _():
            panels[k + 1, c, q] = val
            ag_own(k + 1, q)
            item_part(k + 1, c, q)

        @pl.when(k == LAYERS - 1)
        def _():
            tot = (panels[0, c, q].astype(F32) + panels[1, c, q].astype(F32) + panels[2, c, q].astype(F32)
                   + val.astype(F32))
            out = (tot / (LAYERS + 1)).astype(BF16)
            outu[q] = out
            user_vec[...] += dot_n(out, onehot_a[q])

    def build_round(i):
        _, t, q = place(i)
        build((2 * t + 1 - y) * SUBS + q)
        build((2 * t + y) * SUBS + q)

    base = (r * RING + c) * (SUBS * BLK)
    ids_a = trip[0:1, :] - base
    item_acc[...] = jnp.zeros_like(item_acc)
    user_vec[...] = jnp.zeros_like(user_vec)

    def is_middle(s):
        return lax.div(s * (DEPTH - 1 - s), 2)

    own_lag = 7 - 2 * is_middle(z)
    sets = SUBS * (LAYERS - 1)

    def gather_events(n):
        odd = lax.rem(n, 2)
        f = 1 - odd
        yy = y + f * (1 - 2 * y)

        lag = n - (own_lag + 3)
        @pl.when(jnp.logical_and(lax.rem(lag + 32, 4) == 0, jnp.logical_and(lag >= 0, lag < 4 * sets)))
        def _():
            m = lax.div(lag, 4)
            k, q = lax.div(m, SUBS) + 1, lax.rem(m, SUBS)
            ag_mate(k, q)
            item_part(k, mate, q)

        for d in range(1, DEPTH):
            for above in (True, False):
                s = z + d if above else z - d
                late = n - (7 - 2 * is_middle(s) + 3 * f + 2 * d)
                ok = jnp.logical_and(s < DEPTH, s >= 0)
                ok = jnp.logical_and(ok, jnp.logical_and(late >= 0, late < 4 * sets))

                @pl.when(jnp.logical_and(ok, lax.rem(late + 64, 4) == 0))
                def _():
                    m = lax.div(late, 4)
                    k, q = lax.div(m, SUBS) + 1, lax.rem(m, SUBS)
                    line_event(k, s, yy, q, above, lambda col, q: item_part(k, col, q))

    for i in range(AHEAD):
        build_round(jnp.int32(i))
        y_begin(jnp.int32(i))
    for i in range(AHEAD, 4):
        build_round(jnp.int32(i))
    deg_sum(3)

    def when_at(n, i):
        return pl.when(n == i)

    def one_round(n, carry):
        @when_at(n, 0)
        def _():
            deg_end(1)

        @when_at(n, 2)
        def _():
            deg_end(2)

        @when_at(n, 4)
        def _():
            deg_end(3)

        @when_at(n, 13)
        def _():
            item_share(0, item_sum(0))

        @when_at(n, 14)
        def _():
            item_end(0)

        @when_at(n, 29)
        def _():
            item_share(1, item_sum(1))

        @when_at(n, 30)
        def _():
            item_end(1)

        @when_at(n, 45)
        def _():
            last_item = item_sum(2)
            tot = (ei_all[0, r].astype(F32) + ei_all[1, r].astype(F32) + ei_all[2, r].astype(F32)
                   + last_item.astype(F32))
            out_item = (tot / (LAYERS + 1)).astype(BF16)
            outi[...] = out_item
            item_share(2, out_item)

        @when_at(n, 46)
        def _():
            item_end(2)
            iota_i = lax.broadcasted_iota(jnp.int32, (BLK, 128), 0) + c * BLK
            hot = jnp.concatenate([(iota_i == trip[1:2, :]).astype(BF16), (iota_i == trip[2:3, :]).astype(BF16)],
                                  axis=1)
            got = dot_n(jnp.concatenate([ei_all[3, q] for q in range(ROWS)], axis=1), hot).astype(BF16)
            for q in range(ROWS):
                pk[q] = got[q * 16:(q + 1) * 16, :]
            col_send(2 * SUBS, lambda cc: pk.at[r], pk_recv.at[c])
            pk_recv[c] = pk[r]

        @when_at(n, 48)
        def _():
            col_wait(2 * SUBS, lambda cc: pk.at[r], lambda cc: pk_recv.at[cc])
            psum = pk_recv[0].astype(F32)
            for q in range(1, RING):
                psum = psum + pk_recv[q].astype(F32)
            picks[r] = psum.astype(BF16)
            row_send(8, lambda rr: picks.at[r], picks.at[r])

        @pl.when(n + AHEAD < LAYERS * ROUNDS)
        def _():
            y_begin(n + AHEAD)

        @pl.when(n < LAYERS * ROUNDS)
        def _():
            y_stage(n)

        @pl.when(jnp.logical_and(is_mid, jnp.logical_and(n >= 2, n < LAYERS * ROUNDS + 2)))
        def _():
            mid_stage(n - 2)
        own = n - own_lag + 3

        @pl.when(jnp.logical_and(lax.rem(own + 4, 4) == 3, jnp.logical_and(own >= 0, own < LAYERS * ROUNDS)))
        def _():
            own_stage(own)
        gather_events(n)

        @pl.when(n < 6)
        def _():
            build_round(2 * n + 4)
            build_round(2 * n + 5)

            @pl.loop(2 * n, 2 * n + 2)
            def _(e):
                first_event(e, lambda s, yy, q, above: line_event(0, s, yy, q, above, nothing))

        @pl.when(jnp.logical_and(n >= 6, n < 12))
        def _():
            @pl.loop(2 * n, 2 * n + 2)
            def _(e):
                first_event(e, lambda s, yy, q, above: line_event(
                    0, s, yy, q, above, lambda col, q: item_part(0, col, q)))

            @pl.loop(2 * n - 12, 2 * n - 10)
            def _(e):
                first_event(e, lambda s, yy, q, above: item_part(0, 2 * s + yy, q))

        @pl.when(jnp.logical_and(n >= 6, n < 10))
        def _():
            item_part(0, c, n - 6)
            item_part(0, mate, n - 6)

        @when_at(n, 12)
        def _():
            item_start(0)

        @when_at(n, 28)
        def _():
            item_start(1)

        @pl.when(jnp.logical_and(n >= 32, n < 32 + SUBS))
        def _():
            iota_u = lax.broadcasted_iota(jnp.int32, (BLK, 128), 0) + (n - 32) * BLK
            onehot_a[n - 32] = (iota_u == ids_a).astype(BF16)

        @when_at(n, 44)
        def _():
            item_start(2)
        return carry
    lax.fori_loop(0, LAYERS * ROUNDS + 4, one_round, 0)

    row_wait(8, lambda rr: picks.at[r], lambda rr: picks.at[rr])
    ea = user_vec[...]
    both = jnp.concatenate([picks[q] for q in range(ROWS)], axis=0).astype(F32)
    margin = (jnp.sum(ea * both[:, 0:128], axis=0, keepdims=True)
              - jnp.sum(ea * both[:, 128:256], axis=0, keepdims=True))
    term = jnp.maximum(-margin, 0.0) + jnp.log1p(jnp.exp(-jnp.abs(margin)))
    mine = jnp.logical_and(ids_a >= 0, ids_a < SUBS * BLK)
    terms[r] = jnp.where(mine, term, 0.0)
    row_send(9, lambda rr: terms.at[r], terms.at[r])
    row_wait(9, lambda rr: terms.at[r], lambda rr: terms.at[rr])
    terms2[c] = terms[0] + terms[1] + terms[2] + terms[3]
    col_send(2 * SUBS + 1, lambda cc: terms2.at[c], terms2.at[c])

    def drain(n, carry):
        k, t, q = place(n)
        y_copy(n).wait_send()

        @pl.when(t != z)
        def _():
            z_up(k, t, q).wait_send()
        return carry
    lax.fori_loop(0, LAYERS * ROUNDS, drain, 0)

    def drain_own(q, carry):
        for k in range(LAYERS):
            ag_y(k, q, c).wait_send()
            for col in (c, mate):
                @pl.when(is_up)
                def _():
                    ag_up(k, col, q).wait_send()

                @pl.when(is_down)
                def _():
                    ag_down2(k, col, q).wait_send()
        return carry
    lax.fori_loop(0, SUBS, drain_own, 0)

    def drain_lines(e, carry):
        d, rest = lax.div(e, 2 * SUBS) + 1, lax.rem(e, 2 * SUBS)
        yy, q = lax.div(rest, SUBS), lax.rem(rest, SUBS)
        for k in range(LAYERS):
            @pl.when(jnp.logical_and(z + d < DEPTH, is_down))
            def _():
                ag_down(k, 2 * (z + d) + yy, q).wait_send()

            @pl.when(jnp.logical_and(z - d >= 0, is_up))
            def _():
                ag_up(k, 2 * (z - d) + yy, q).wait_send()
        return carry
    lax.fori_loop(0, 6 * SUBS, drain_lines, 0)

    col_wait(2 * SUBS + 1, lambda cc: terms2.at[c], lambda cc: terms2.at[cc])
    tsum = terms2[0]
    for q in range(1, RING):
        tsum = tsum + terms2[q]
    loss[...] = jnp.broadcast_to(jnp.sum(tsum, axis=1, keepdims=True) / tsum.shape[1], loss.shape)


def solution(mesh):
    def local_prog(mask_blk, user_shard, item_shard, triples):
        vmem = pl.BlockSpec(memory_space=pltpu.VMEM)
        dma = pltpu.SemaphoreType.DMA
        outu, outi, loss = pl.pallas_call(
            kernel,
            out_shape=(jax.ShapeDtypeStruct((SUBS, DIM, BLK), BF16),
                       jax.ShapeDtypeStruct((DIM, 128), BF16),
                       jax.ShapeDtypeStruct((8, 128), F32)),
            in_specs=[pl.BlockSpec(memory_space=pl.ANY), vmem, vmem, vmem],
            out_specs=(vmem, vmem, vmem),
            scratch_shapes=[
                pltpu.VMEM((RING * SUBS, BLK, BLK), BF16),
                pltpu.VMEM((MASK_BUFS, BLK, BLK), jnp.int32),
                dma((MASK_BUFS,)),
                pltpu.VMEM((LAYERS, RING, SUBS, DIM, BLK), BF16),
                pltpu.VMEM((LAYERS + 1, ROWS, DIM, 128), BF16),
                pltpu.VMEM((LAYERS, DIM, BLK), F32),
                pltpu.VMEM((LAYERS, ROWS, DIM, 128), F32),
                pltpu.VMEM((LAYERS, ROWS, DIM, 128), F32),
                pltpu.VMEM((LAYERS, DEPTH, SUBS, DIM, BLK), F32),
                pltpu.VMEM((LAYERS, DEPTH, SUBS, DIM, BLK), F32),
                pltpu.VMEM((LAYERS, DEPTH + 1, SUBS, DIM, BLK), F32),
                pltpu.VMEM((8, BLK), F32),
                pltpu.VMEM((RING * SUBS, 1, BLK), F32),
                pltpu.VMEM((RING, SUBS, 1, BLK), F32),
                pltpu.VMEM((RING * SUBS, 1, BLK), F32),
                pltpu.VMEM((1, BLK), F32),
                pltpu.VMEM((ROWS, 1, BLK), F32),
                pltpu.VMEM((1, BLK), F32),
                pltpu.VMEM((SUBS, BLK, 128), BF16),
                pltpu.VMEM((ROWS, 16, 256), BF16),
                pltpu.VMEM((RING, 16, 256), BF16),
                pltpu.VMEM((ROWS, 16, 256), BF16),
                pltpu.VMEM((DIM, 128), F32),
                pltpu.VMEM((ROWS, 1, 128), F32),
                pltpu.VMEM((RING, 1, 128), F32),
                dma((LAYERS, DEPTH, SUBS)), dma((LAYERS, DEPTH, SUBS)),
                dma((LAYERS, DEPTH, SUBS)), dma((LAYERS, DEPTH + 1, SUBS)),
                dma((LAYERS, SUBS)), dma((LAYERS, RING, SUBS)), dma((LAYERS, 2, SUBS)), dma((LAYERS, RING, SUBS)),
                dma((10, ROWS)), dma((10, ROWS)),
                dma((2 * SUBS + 2, RING)), dma((2 * SUBS + 2, RING)),
            ],
            compiler_params=pltpu.CompilerParams(
                collective_id=0, has_side_effects=True, vmem_limit_bytes=61 * 1024 * 1024),
            name="propagate",
        )(mask_blk, user_shard.T, item_shard.T, triples.T)
        out_user = jnp.concatenate([outu[q] for q in range(SUBS)], axis=1).T
        return out_user, outi.T, loss[0, 0]

    return jax.shard_map(local_prog, mesh=mesh,
                         in_specs=(P("row", "col"), P(("row", "col"), None), P(("col", "row"), None), P(None, None)),
                         out_specs=(P(("row", "col"), None), P(("col", "row"), None), P()), check_vma=False)
```

time: 216 us -> 198 us (0.917)
  Pallas kernels: 211 us -> 193 us
    pallas_call x1, Pallas kernels: 211 us -> 193 us  [local_prog(): pl.pallas_call(kernel, out_shape=(jax.ShapeDtypeStruct((SUBS, DIM, BLK),...]
where the time goes in v3:
time: 198 us
  Pallas kernels  193 us (97%)
  local copies, waits for them, and re-layouts  3.46 us (2%)
    pallas_call x1, Pallas kernels, local_prog(): pl.pallas_call(kernel, out_shape=(jax.ShapeDtypeStruct((SUBS, DIM, BLK),...  193 us

profile of v3, /device:TPU:0, one launch (start us, length us, event | category | flops | bytes accessed | tf_op | source)
XLA Modules:
  0.0 197.9 jit_solution(10962337358575320353)
XLA Ops:
  0.6 193.1 %propagate.1 = (bf16[4,64,512]{2,1,0:T(8,128)(2,1)}, bf16[64,128]{1,0:T(8,128)(2,1)}, f32[8,128]{1,0:T(8,128)}) custom-call(s32[16384,512]{1,0:T(8,128)} %mask_hbm.1, bf16[64,2048]{1,0:T(8,128)(2,1)} %bitcast.15, bf16[64,128]{1,0:T(8,128)(2,1)} %bitcast.16, s32[3,128]{1,0:T(4,128)} %bitcast.18), custom_call_target="tpu_custom_call" | custom-call | tf_op jit(solution)/shard_map/propagate/pallas_call | solution.py:574
  193.7 1.2 slice.19
  194.9 1.0 slice_bitcast_fusion.3
  195.8 0.7 maximum_bitcast_fusion
  196.6 1.3 copy.8

commit v4 on v3

--- a/solution.py
+++ b/solution.py
@@ -11,6 +11,7 @@
 DEPTH = 4
 ROUNDS = 16
 AHEAD = 2
+Y_SEMS = 8
 SUBS = 4
 DIM = 64
 BLK = 512
@@ -34,7 +35,7 @@
            ysend, yrecv, zin,
            colsum, deg_part, deg_recv, scale_u, itemdeg, itemdeg_recv, scale_v,
            onehot_a, pk, pk_recv, picks, user_vec, terms, terms2,
-           y_ss, y_rs, z_ss, z_rs, ag_sy, ag_s1, ag_s2, ag_rs,
+           y_ss, y_rs, z_ss, z_rs, ag_sy, ag_su, ag_sd, ag_rs,
            row_ss, row_rs, col_ss, col_rs):
     c = lax.axis_index("col")
     r = lax.axis_index("row")
@@ -65,21 +66,20 @@
         return pltpu.make_async_remote_copy(src_ref=src, dst_ref=dst, send_sem=ss, recv_sem=rs,
                                             device_id=(col, r), device_id_type=MESH)
 
+    def ag_rs_of(k, col, q):
+        return ag_rs.at[lax.div(k + 1, 2), col, q]
+
     def ag_y(k, q, col):
         ref = panels.at[k, col, q]
-        return remote(ref, ref, ag_sy.at[k, q], ag_rs.at[k, col, q], mate)
+        return remote(ref, ref, ag_sy, ag_rs_of(k, col, q), mate)
 
     def ag_up(k, col, q):
         ref = panels.at[k, col, q]
-        return remote(ref, ref, ag_s1.at[k, col, q], ag_rs.at[k, col, q], c + 2)
+        return remote(ref, ref, ag_su, ag_rs_of(k, col, q), c + 2)
 
     def ag_down(k, col, q):
         ref = panels.at[k, col, q]
-        return remote(ref, ref, ag_s1.at[k, col, q], ag_rs.at[k, col, q], c - 2)
-
-    def ag_down2(k, col, q):
-        ref = panels.at[k, col, q]
-        return remote(ref, ref, ag_s2.at[k, lax.rem(col, 2), q], ag_rs.at[k, col, q], c - 2)
+        return remote(ref, ref, ag_sd, ag_rs_of(k, col, q), c - 2)
 
     def ag_both(k, col, q):
         @pl.when(is_up)
@@ -88,7 +88,7 @@
 
         @pl.when(is_down)
         def _():
-            ag_down2(k, col, q).start()
+            ag_down(k, col, q).start()
 
     def ag_own(k, q):
         ag_y(k, q, c).start()
@@ -132,27 +132,25 @@
 
     def row_send(u, src, dst):
         for rr in row_peers:
-            pltpu.make_async_remote_copy(src_ref=src(rr), dst_ref=dst, send_sem=row_ss.at[u, rr],
-                                         recv_sem=row_rs.at[u, r], device_id=(c, rr), device_id_type=MESH).start()
-
-    def row_wait(u, src, dst):
+            pltpu.make_async_remote_copy(src_ref=src(rr), dst_ref=dst, send_sem=row_ss.at[u], recv_sem=row_rs.at[u],
+                                         device_id=(c, rr), device_id_type=MESH).start()
+
+    def row_wait(u, ref):
         with jax.named_scope("row_wait_%d" % u):
-            for rr in row_peers:
-                cp = pltpu.make_async_remote_copy(src_ref=src(rr), dst_ref=dst(rr), send_sem=row_ss.at[u, rr],
-                                                  recv_sem=row_rs.at[u, rr], device_id=(c, rr), device_id_type=MESH)
-                cp.wait_recv()
-                cp.wait_send()
+            cp = pltpu.make_async_remote_copy(src_ref=ref, dst_ref=ref, send_sem=row_ss.at[u], recv_sem=row_rs.at[u],
+                                              device_id=(c, row_peers[0]), device_id_type=MESH)
+            cp.wait_recv()
+            cp.wait_send()
 
     def col_send(u, src, dst):
         for cc in col_peers:
-            remote(src(cc), dst, col_ss.at[u, cc], col_rs.at[u, c], cc).start()
-
-    def col_wait(u, src, dst):
+            remote(src(cc), dst, col_ss.at[u], col_rs.at[u], cc).start()
+
+    def col_wait(u, ref):
         with jax.named_scope("col_wait_%d" % u):
-            for cc in col_peers:
-                cp = remote(src(cc), dst(cc), col_ss.at[u, cc], col_rs.at[u, cc], cc)
-                cp.wait_recv()
-                cp.wait_send()
+            cp = remote(ref, ref, col_ss.at[u], col_rs.at[u], mate)
+            cp.wait_recv()
+            cp.wait_send()
 
     ones = jnp.ones((16, BLK), BF16)
     colsum[...] = jnp.zeros_like(colsum)
@@ -178,7 +176,7 @@
         deg_recv[c, q] = deg_part[c * SUBS + q]
 
     def deg_sum(q):
-        col_wait(q, lambda cc: deg_part.at[cc * SUBS + q], lambda cc: deg_recv.at[cc, q])
+        col_wait(q, deg_part.at[pl.ds(0, RING - 1)])
         du = deg_recv[0, q]
         for cc in range(1, RING):
             du = du + deg_recv[cc, q]
@@ -186,11 +184,14 @@
         col_send(SUBS + q, lambda cc: scale_u.at[c * SUBS + q], scale_u.at[c * SUBS + q])
 
     def deg_end(q):
-        col_wait(SUBS + q, lambda cc: scale_u.at[c * SUBS + q], lambda cc: scale_u.at[cc * SUBS + q])
+        col_wait(SUBS + q, deg_part.at[pl.ds(0, RING - 1)])
 
     def mask_quarter(q):
         with jax.named_scope("mask"):
             lax.fori_loop(RING * q, RING * (q + 1), mask_block, 0)
+
+    def early_event(e):
+        first_event(jnp.int32(e), lambda s, yy, q, above: line_event(0, s, yy, q, above, lambda col, q: None))
 
     mask_quarter(0)
     for q in range(SUBS):
@@ -199,28 +200,29 @@
     with jax.named_scope("entry"):
         pl.semaphore_wait(barrier, (ROWS - 1) + (RING - 1))
     deg_send(0)
-    for q in range(SUBS):
-        ag_own(0, q)
+    ag_own(0, 0)
+    ag_own(0, 1)
     row_send(0, lambda rr: ei_all.at[0, r], ei_all.at[0, r])
     mask_quarter(1)
     deg_send(1)
+    ag_own(0, 2)
     mask_quarter(2)
     deg_send(2)
+    ag_own(0, 3)
     deg_sum(0)
+    for q in range(2):
+        ag_mate(0, q)
+        early_event(q)
     mask_quarter(3)
     itemdeg[...] = jnp.sum(colsum[...], axis=0, keepdims=True)
     row_send(1, lambda rr: itemdeg, itemdeg_recv.at[r])
     deg_send(3)
     itemdeg_recv[r] = itemdeg[...]
-    nothing = lambda col, q: None
     deg_sum(1)
-    for q in range(SUBS):
-        ag_mate(0, q)
-    deg_sum(2)
-    row_wait(1, lambda rr: itemdeg, lambda rr: itemdeg_recv.at[rr])
+    row_wait(1, itemdeg_recv.at[pl.ds(0, ROWS - 1)])
     dv = itemdeg_recv[0] + itemdeg_recv[1] + itemdeg_recv[2] + itemdeg_recv[3]
     scale_v[...] = lax.rsqrt(jnp.maximum(dv, 1.0))
-    row_wait(0, lambda rr: ei_all.at[0, r], lambda rr: ei_all.at[0, rr])
+    row_wait(0, ei_all.at[0, pl.ds(0, ROWS - 1)])
     deg_end(0)
 
     def build(b):
@@ -245,7 +247,7 @@
         item_recv[k, r] = item_send[k, r]
 
     def item_sum(k):
-        row_wait(2 + 2 * k, lambda rr: item_send.at[k, rr], lambda rr: item_recv.at[k, rr])
+        row_wait(2 + 2 * k, item_send.at[k, pl.ds(0, ROWS - 1)])
         tot = item_recv[k, 0] + item_recv[k, 1] + item_recv[k, 2] + item_recv[k, 3]
         return tot.astype(BF16)
 
@@ -254,16 +256,21 @@
         row_send(3 + 2 * k, lambda rr: ei_all.at[k + 1, r], ei_all.at[k + 1, r])
 
     def item_end(k):
-        row_wait(3 + 2 * k, lambda rr: ei_all.at[k + 1, r], lambda rr: ei_all.at[k + 1, rr])
+        row_wait(3 + 2 * k, ei_all.at[k + 1, pl.ds(0, ROWS - 1)])
 
     def place(n):
-        k, q, g = lax.div(n, ROUNDS), lax.rem(lax.div(n, DEPTH), SUBS), lax.rem(n, DEPTH)
+        k, i = lax.div(n, ROUNDS), lax.rem(n, ROUNDS)
+        last, own = lax.div(k, LAYERS - 1), lax.div(i, 12)
+        q, g = lax.div(i, 4), lax.rem(i, 4)
+        q_last = (1 - own) * lax.div(i, 3) + own * (i - 12)
+        g_last = (1 - own) * lax.rem(i, 3) + own * 3
+        q, g = q + last * (q_last - q), g + last * (g_last - g)
         pw = 1 + 3 * g + 9 * lax.div(g * (g - 1), 2) + 27 * lax.div(g * (g - 1) * (g - 2), 6)
         return k, lax.rem(lax.div(27 + 48 * z + 57 * lax.div(z, 2), pw), DEPTH), q
 
     def y_copy(n):
         k, t, q = place(n)
-        return remote(ysend.at[k, t, q], yrecv.at[k, t, q], y_ss.at[k, t, q], y_rs.at[k, t, q], mate)
+        return remote(ysend.at[k, t, q], yrecv.at[k, t, q], y_ss, y_rs.at[lax.rem(n, Y_SEMS)], mate)
 
     def y_begin(n):
         k, t, q = place(n)
@@ -271,15 +278,15 @@
         y_copy(n).start()
 
     def z_up(k, t, q):
-        return remote(yrecv.at[k, t, q], zin.at[k, t, q], z_ss.at[k, t, q], z_rs.at[k, t, q], c + 2)
+        return remote(yrecv.at[k, t, q], zin.at[k, t, q], z_ss, z_rs.at[t, q], c + 2)
 
     def z_down(k, t, q):
         to = t + lax.div(2 - (z - 1 - t), 2) * (DEPTH - t)
-        return remote(yrecv.at[k, t, q], zin.at[k, to, q], z_ss.at[k, t, q], z_rs.at[k, to, q], c - 2)
+        return remote(yrecv.at[k, t, q], zin.at[k, to, q], z_ss, z_rs.at[to, q], c - 2)
 
     def z_add(k, t, at, q):
         with jax.named_scope("rs_z"):
-            remote(yrecv.at[k, t, q], zin.at[k, at, q], z_ss.at[k, t, q], z_rs.at[k, at, q], mate).wait_recv()
+            remote(yrecv.at[k, t, q], zin.at[k, at, q], z_ss, z_rs.at[at, q], mate).wait_recv()
         yrecv[k, t, q] = yrecv[k, t, q] + zin[k, at, q]
 
     def z_send(k, t, q):
@@ -383,39 +390,125 @@
         y_begin(jnp.int32(i))
     for i in range(AHEAD, 4):
         build_round(jnp.int32(i))
-    deg_sum(3)
+    deg_sum(2)
+    for q in range(2, SUBS):
+        ag_mate(0, q)
+        early_event(q)
 
     def when_at(n, i):
         return pl.when(n == i)
 
     def one_round(n, carry):
-        @when_at(n, 0)
+        @when_at(n, 1)
         def _():
             deg_end(1)
-
-        @when_at(n, 2)
+            deg_sum(3)
+
+        @when_at(n, 3)
         def _():
             deg_end(2)
 
-        @when_at(n, 4)
+        @when_at(n, 5)
         def _():
             deg_end(3)
 
         @when_at(n, 13)
         def _():
+            item_end(0)
+
+        @when_at(n, 29)
+        def _():
+            item_share(1, item_sum(1))
+
+        @when_at(n, 30)
+        def _():
+            item_end(1)
+
+        @pl.when(n + AHEAD < LAYERS * ROUNDS)
+        def _():
+            y_begin(n + AHEAD)
+
+        y_stage(n)
+
+        @pl.when(jnp.logical_and(is_mid, n >= 2))
+        def _():
+            mid_stage(n - 2)
+        own = n - own_lag + 3
+
+        @pl.when(jnp.logical_and(lax.rem(own + 4, 4) == 3, jnp.logical_and(own >= 0, own < 2 * ROUNDS)))
+        def _():
+            own_stage(own)
+        gather_events(n)
+
+        @when_at(n, 47)
+        def _():
+            col_wait(2 * SUBS, pk_recv.at[pl.ds(0, RING - 1)])
+            psum = pk_recv[0].astype(F32)
+            for q in range(1, RING):
+                psum = psum + pk_recv[q].astype(F32)
+            picks[r] = psum.astype(BF16)
+            row_send(8, lambda rr: picks.at[r], picks.at[r])
+
+        @pl.when(n >= LAYERS * ROUNDS - SUBS)
+        def _():
+            own_stage(n)
+
+        @pl.when(jnp.logical_and(n >= 1, n < 7))
+        def _():
+            build_round(2 * n + 2)
+            build_round(2 * n + 3)
+
+        @pl.when(n < 6)
+        def _():
+            early_event(2 * n + 4)
+            early_event(2 * n + 5)
+
+        def late_event(e):
+            first_event(e, lambda s, yy, q, above: line_event(
+                0, s, yy, q, above, lambda col, q: item_part(0, col, q)))
+
+        def old_event(e):
+            first_event(e, lambda s, yy, q, above: item_part(0, 2 * s + yy, q))
+
+        @pl.when(jnp.logical_and(n >= 6, n < 11))
+        def _():
+            e = 16 + (n - 6) + lax.div(n - 6, 3) + lax.div(n - 6, 4)
+            late_event(e)
+
+            @pl.when(n >= 8)
+            def _():
+                late_event(e + 1)
+
+        @pl.when(jnp.logical_and(n >= 1, n < 9))
+        def _():
+            q, side = lax.div(n - 1, 2), lax.rem(n - 1, 2)
+            item_part(0, c + side * (mate - c), q)
+            old_event(q + 4 * side)
+
+        @pl.when(jnp.logical_and(n >= 4, n < 11))
+        def _():
+            old_event(n + 4 + lax.div(n, 9))
+
+            @pl.when(n == 8)
+            def _():
+                old_event(n + 5)
+
+        @when_at(n, 10)
+        def _():
+            item_start(0)
+
+        @when_at(n, 11)
+        def _():
             item_share(0, item_sum(0))
 
-        @when_at(n, 14)
-        def _():
-            item_end(0)
-
-        @when_at(n, 29)
-        def _():
-            item_share(1, item_sum(1))
-
-        @when_at(n, 30)
-        def _():
-            item_end(1)
+        @when_at(n, 28)
+        def _():
+            item_start(1)
+
+        @pl.when(jnp.logical_and(n >= 32, n < 32 + SUBS))
+        def _():
+            iota_u = lax.broadcasted_iota(jnp.int32, (BLK, 128), 0) + (n - 32) * BLK
+            onehot_a[n - 32] = (iota_u == ids_a).astype(BF16)
 
         @when_at(n, 45)
         def _():
@@ -438,78 +531,13 @@
             col_send(2 * SUBS, lambda cc: pk.at[r], pk_recv.at[c])
             pk_recv[c] = pk[r]
 
-        @when_at(n, 48)
-        def _():
-            col_wait(2 * SUBS, lambda cc: pk.at[r], lambda cc: pk_recv.at[cc])
-            psum = pk_recv[0].astype(F32)
-            for q in range(1, RING):
-                psum = psum + pk_recv[q].astype(F32)
-            picks[r] = psum.astype(BF16)
-            row_send(8, lambda rr: picks.at[r], picks.at[r])
-
-        @pl.when(n + AHEAD < LAYERS * ROUNDS)
-        def _():
-            y_begin(n + AHEAD)
-
-        @pl.when(n < LAYERS * ROUNDS)
-        def _():
-            y_stage(n)
-
-        @pl.when(jnp.logical_and(is_mid, jnp.logical_and(n >= 2, n < LAYERS * ROUNDS + 2)))
-        def _():
-            mid_stage(n - 2)
-        own = n - own_lag + 3
-
-        @pl.when(jnp.logical_and(lax.rem(own + 4, 4) == 3, jnp.logical_and(own >= 0, own < LAYERS * ROUNDS)))
-        def _():
-            own_stage(own)
-        gather_events(n)
-
-        @pl.when(n < 6)
-        def _():
-            build_round(2 * n + 4)
-            build_round(2 * n + 5)
-
-            @pl.loop(2 * n, 2 * n + 2)
-            def _(e):
-                first_event(e, lambda s, yy, q, above: line_event(0, s, yy, q, above, nothing))
-
-        @pl.when(jnp.logical_and(n >= 6, n < 12))
-        def _():
-            @pl.loop(2 * n, 2 * n + 2)
-            def _(e):
-                first_event(e, lambda s, yy, q, above: line_event(
-                    0, s, yy, q, above, lambda col, q: item_part(0, col, q)))
-
-            @pl.loop(2 * n - 12, 2 * n - 10)
-            def _(e):
-                first_event(e, lambda s, yy, q, above: item_part(0, 2 * s + yy, q))
-
-        @pl.when(jnp.logical_and(n >= 6, n < 10))
-        def _():
-            item_part(0, c, n - 6)
-            item_part(0, mate, n - 6)
-
-        @when_at(n, 12)
-        def _():
-            item_start(0)
-
-        @when_at(n, 28)
-        def _():
-            item_start(1)
-
-        @pl.when(jnp.logical_and(n >= 32, n < 32 + SUBS))
-        def _():
-            iota_u = lax.broadcasted_iota(jnp.int32, (BLK, 128), 0) + (n - 32) * BLK
-            onehot_a[n - 32] = (iota_u == ids_a).astype(BF16)
-
         @when_at(n, 44)
         def _():
             item_start(2)
         return carry
-    lax.fori_loop(0, LAYERS * ROUNDS + 4, one_round, 0)
-
-    row_wait(8, lambda rr: picks.at[r], lambda rr: picks.at[rr])
+    lax.fori_loop(0, LAYERS * ROUNDS, one_round, 0)
+
+    row_wait(8, picks.at[pl.ds(0, ROWS - 1)])
     ea = user_vec[...]
     both = jnp.concatenate([picks[q] for q in range(ROWS)], axis=0).astype(F32)
     margin = (jnp.sum(ea * both[:, 0:128], axis=0, keepdims=True)
@@ -518,53 +546,36 @@
     mine = jnp.logical_and(ids_a >= 0, ids_a < SUBS * BLK)
     terms[r] = jnp.where(mine, term, 0.0)
     row_send(9, lambda rr: terms.at[r], terms.at[r])
-    row_wait(9, lambda rr: terms.at[r], lambda rr: terms.at[rr])
+    row_wait(9, terms.at[pl.ds(0, ROWS - 1)])
     terms2[c] = terms[0] + terms[1] + terms[2] + terms[3]
     col_send(2 * SUBS + 1, lambda cc: terms2.at[c], terms2.at[c])
 
-    def drain(n, carry):
-        k, t, q = place(n)
-        y_copy(n).wait_send()
-
-        @pl.when(t != z)
-        def _():
-            z_up(k, t, q).wait_send()
-        return carry
-    lax.fori_loop(0, LAYERS * ROUNDS, drain, 0)
-
-    def drain_own(q, carry):
-        for k in range(LAYERS):
-            ag_y(k, q, c).wait_send()
-            for col in (c, mate):
-                @pl.when(is_up)
-                def _():
-                    ag_up(k, col, q).wait_send()
-
-                @pl.when(is_down)
-                def _():
-                    ag_down2(k, col, q).wait_send()
-        return carry
-    lax.fori_loop(0, SUBS, drain_own, 0)
-
-    def drain_lines(e, carry):
-        d, rest = lax.div(e, 2 * SUBS) + 1, lax.rem(e, 2 * SUBS)
-        yy, q = lax.div(rest, SUBS), lax.rem(rest, SUBS)
-        for k in range(LAYERS):
-            @pl.when(jnp.logical_and(z + d < DEPTH, is_down))
-            def _():
-                ag_down(k, 2 * (z + d) + yy, q).wait_send()
-
-            @pl.when(jnp.logical_and(z - d >= 0, is_up))
-            def _():
-                ag_up(k, 2 * (z - d) + yy, q).wait_send()
-        return carry
-    lax.fori_loop(0, 6 * SUBS, drain_lines, 0)
-
-    col_wait(2 * SUBS + 1, lambda cc: terms2.at[c], lambda cc: terms2.at[cc])
+    def drain(ref, sem):
+        remote(ref, ref, sem, y_rs.at[0], mate).wait_send()
+
+    drain(ysend, y_ss)
+    drain(yrecv.at[:, pl.ds(0, DEPTH - 1)], z_ss)
+    drain(panels.at[:, pl.ds(0, 1)], ag_sy)
+    for at in range(DEPTH):
+        @pl.when(z == at)
+        def _():
+            if at < DEPTH - 1:
+                drain(panels.at[:, pl.ds(0, 2 * (at + 1))], ag_su)
+            if at > 0:
+                drain(panels.at[:, pl.ds(0, 2 * (DEPTH - at))], ag_sd)
+
+    col_wait(2 * SUBS + 1, terms2.at[pl.ds(0, RING - 1)])
     tsum = terms2[0]
     for q in range(1, RING):
         tsum = tsum + terms2[q]
     loss[...] = jnp.broadcast_to(jnp.sum(tsum, axis=1, keepdims=True) / tsum.shape[1], loss.shape)
+
+
+def deliver(outu, outi, loss, to_user, to_item, to_loss):
+    for q in range(SUBS):
+        to_user[:, q * BLK:(q + 1) * BLK] = outu[q]
+    to_item[...] = outi[...]
+    to_loss[...] = loss[0:1, 0:1]
 
 
 def solution(mesh):
@@ -604,18 +615,22 @@
                 pltpu.VMEM((DIM, 128), F32),
                 pltpu.VMEM((ROWS, 1, 128), F32),
                 pltpu.VMEM((RING, 1, 128), F32),
-                dma((LAYERS, DEPTH, SUBS)), dma((LAYERS, DEPTH, SUBS)),
-                dma((LAYERS, DEPTH, SUBS)), dma((LAYERS, DEPTH + 1, SUBS)),
-                dma((LAYERS, SUBS)), dma((LAYERS, RING, SUBS)), dma((LAYERS, 2, SUBS)), dma((LAYERS, RING, SUBS)),
-                dma((10, ROWS)), dma((10, ROWS)),
-                dma((2 * SUBS + 2, RING)), dma((2 * SUBS + 2, RING)),
+                dma, dma((Y_SEMS,)), dma, dma((DEPTH + 1, SUBS)),
+                dma, dma, dma, dma((2, RING, SUBS)),
+                dma((10,)), dma((10,)), dma((2 * SUBS + 2,)), dma((2 * SUBS + 2,)),
             ],
             compiler_params=pltpu.CompilerParams(
                 collective_id=0, has_side_effects=True, vmem_limit_bytes=61 * 1024 * 1024),
             name="propagate",
         )(mask_blk, user_shard.T, item_shard.T, triples.T)
-        out_user = jnp.concatenate([outu[q] for q in range(SUBS)], axis=1).T
-        return out_user, outi.T, loss[0, 0]
+        out_user, out_item, mean = pl.pallas_call(
+            deliver,
+            out_shape=(jax.ShapeDtypeStruct((DIM, SUBS * BLK), BF16),
+                       jax.ShapeDtypeStruct((DIM, 128), BF16),
+                       jax.ShapeDtypeStruct((1, 1), F32)),
+            in_specs=[vmem, vmem, vmem], out_specs=(vmem, vmem, vmem), name="deliver",
+        )(outu, outi, loss)
+        return out_user.T, out_item.T, mean[0, 0]
 
     return jax.shard_map(local_prog, mesh=mesh,
                          in_specs=(P("row", "col"), P(("row", "col"), None), P(("col", "row"), None), P(None, None)),

time: 198 us -> 186 us (0.939)
  Pallas kernels: 193 us -> 185 us
  local copies, waits for them, and re-layouts: 3.46 us -> 0 us
    pallas_call x1, Pallas kernels: 193 us -> 184 us  [local_prog(): pl.pallas_call(kernel, out_shape=(jax.ShapeDtypeStruct((SUBS, DIM, BLK),...]
where the time goes in v4:
time: 186 us
  Pallas kernels  185 us (99%)
    pallas_call x1, Pallas kernels, local_prog(): pl.pallas_call(kernel, out_shape=(jax.ShapeDtypeStruct((SUBS, DIM, BLK),...  184 us

profile of v4, /device:TPU:0, one launch (start us, length us, event | category | flops | bytes accessed | tf_op | source)
XLA Modules:
  0.0 186.0 jit_solution(9553695254086586952)
XLA Ops:
  0.6 183.7 %propagate.1 = (bf16[4,64,512]{2,1,0:T(8,128)(2,1)}, bf16[64,128]{1,0:T(8,128)(2,1)}, f32[8,128]{1,0:T(8,128)}) custom-call(s32[16384,512]{1,0:T(8,128)} %mask_hbm.1, bf16[64,2048]{1,0:T(8,128)(2,1)} %bitcast.6, bf16[64,128]{1,0:T(8,128)(2,1)} %bitcast.7, s32[3,128]{1,0:T(4,128)} %bitcast.8), custom_call_target="tpu_custom_call" | custom-call | tf_op jit(solution)/shard_map/propagate/pallas_call | solution.py:585
  184.3 1.7 deliver.1

commit v5 on v4

--- a/solution.py
+++ b/solution.py
@@ -29,8 +29,8 @@
     return lax.dot_general(lhs, rhs, (((1,), (0,)), ((), ())), preferred_element_type=F32)
 
 
-def kernel(mask_hbm, euT, eiT, trip, outu, outi, loss,
-           adj, mbuf, msem,
+def kernel(mask_hbm, euT, eiT, trip_hbm, outu_hbm, outi_hbm, loss,
+           adj, mbuf, msem, io_sem, trip, outu, outi,
            panels, ei_all, item_acc, item_send, item_recv,
            ysend, yrecv, zin,
            colsum, deg_part, deg_recv, scale_u, itemdeg, itemdeg_recv, scale_v,
@@ -56,6 +56,16 @@
     for i in range(MASK_BUFS):
         mask_copy(jnp.int32(i)).start()
 
+    def table_in(q):
+        return pltpu.make_async_copy(euT.at[:, pl.ds(q * BLK, BLK)], panels.at[0, c, q], io_sem.at[q])
+
+    item_in = pltpu.make_async_copy(eiT, ei_all.at[0, r], io_sem.at[SUBS])
+    trip_in = pltpu.make_async_copy(trip_hbm, trip, io_sem.at[SUBS + 1])
+    for q in range(SUBS):
+        table_in(q).start()
+    item_in.start()
+    trip_in.start()
+
     barrier = pltpu.get_barrier_semaphore()
     for rr in row_peers:
         pl.semaphore_signal(barrier, inc=1, device_id=(c, rr), device_id_type=MESH)
@@ -195,8 +205,9 @@
 
     mask_quarter(0)
     for q in range(SUBS):
-        panels[0, c, q] = euT[:, q * BLK:(q + 1) * BLK]
-    ei_all[0, r] = eiT[...]
+        table_in(q).wait()
+    item_in.wait()
+    trip_in.wait()
     with jax.named_scope("entry"):
         pl.semaphore_wait(barrier, (ROWS - 1) + (RING - 1))
     deg_send(0)
@@ -317,6 +328,11 @@
             z_add(k, t, t, q)
             z_send(k, t, q)
 
+    def table_out(q):
+        return pltpu.make_async_copy(outu.at[q], outu_hbm.at[q], io_sem.at[q])
+
+    item_out = pltpu.make_async_copy(outi, outi_hbm, io_sem.at[SUBS])
+
     def own_stage(n):
         k, _, q = place(n)
 
@@ -341,6 +357,7 @@
                    + val.astype(F32))
             out = (tot / (LAYERS + 1)).astype(BF16)
             outu[q] = out
+            table_out(q).start()
             user_vec[...] += dot_n(out, onehot_a[q])
 
     def build_round(i):
@@ -359,31 +376,27 @@
     own_lag = 7 - 2 * is_middle(z)
     sets = SUBS * (LAYERS - 1)
 
-    def gather_events(n):
-        odd = lax.rem(n, 2)
-        f = 1 - odd
-        yy = y + f * (1 - 2 * y)
-
-        lag = n - (own_lag + 3)
-        @pl.when(jnp.logical_and(lax.rem(lag + 32, 4) == 0, jnp.logical_and(lag >= 0, lag < 4 * sets)))
-        def _():
-            m = lax.div(lag, 4)
-            k, q = lax.div(m, SUBS) + 1, lax.rem(m, SUBS)
+    def gather_set(late, event):
+        @pl.when(jnp.logical_and(lax.rem(late + 64, 8) == 0, jnp.logical_and(late >= 0, late < 8 * sets)))
+        def _():
+            m = lax.div(late, 8)
+            event(lax.div(m, SUBS) + 1, lax.rem(m, SUBS))
+
+    def gather_mate(half):
+        def event(k, q):
             ag_mate(k, q)
             item_part(k, mate, q)
-
-        for d in range(1, DEPTH):
-            for above in (True, False):
-                s = z + d if above else z - d
-                late = n - (7 - 2 * is_middle(s) + 3 * f + 2 * d)
-                ok = jnp.logical_and(s < DEPTH, s >= 0)
-                ok = jnp.logical_and(ok, jnp.logical_and(late >= 0, late < 4 * sets))
-
-                @pl.when(jnp.logical_and(ok, lax.rem(late + 64, 4) == 0))
-                def _():
-                    m = lax.div(late, 4)
-                    k, q = lax.div(m, SUBS) + 1, lax.rem(m, SUBS)
-                    line_event(k, s, yy, q, above, lambda col, q: item_part(k, col, q))
+        gather_set(half - (2 * own_lag + 6), event)
+
+    def gather_line(half, d, f):
+        for above in (True, False):
+            s = z + d if above else z - d
+
+            @pl.when(jnp.logical_and(s < DEPTH, s >= 0))
+            def _():
+                gather_set(half - (2 * (7 - 2 * is_middle(s)) + 3 * d + (6 if f else 1)),
+                           lambda k, q: line_event(k, s, 1 - y if f else y, q, above,
+                                                   lambda col, q: item_part(k, col, q)))
 
     for i in range(AHEAD):
         build_round(jnp.int32(i))
@@ -416,18 +429,13 @@
         def _():
             item_end(0)
 
-        @when_at(n, 29)
-        def _():
-            item_share(1, item_sum(1))
-
-        @when_at(n, 30)
-        def _():
-            item_end(1)
-
         @pl.when(n + AHEAD < LAYERS * ROUNDS)
         def _():
             y_begin(n + AHEAD)
 
+        gather_mate(2 * n)
+        for d, f in ((1, 0), (2, 1), (3, 0)):
+            gather_line(2 * n, d, f)
         y_stage(n)
 
         @pl.when(jnp.logical_and(is_mid, n >= 2))
@@ -438,9 +446,10 @@
         @pl.when(jnp.logical_and(lax.rem(own + 4, 4) == 3, jnp.logical_and(own >= 0, own < 2 * ROUNDS)))
         def _():
             own_stage(own)
-        gather_events(n)
-
-        @when_at(n, 47)
+        for d, f in ((1, 1), (2, 0), (3, 1)):
+            gather_line(2 * n + 1, d, f)
+
+        @when_at(n, 46)
         def _():
             col_wait(2 * SUBS, pk_recv.at[pl.ds(0, RING - 1)])
             psum = pk_recv[0].astype(F32)
@@ -501,25 +510,34 @@
         def _():
             item_share(0, item_sum(0))
 
-        @when_at(n, 28)
+        @when_at(n, 26)
         def _():
             item_start(1)
+
+        @when_at(n, 27)
+        def _():
+            item_share(1, item_sum(1))
+
+        @when_at(n, 29)
+        def _():
+            item_end(1)
 
         @pl.when(jnp.logical_and(n >= 32, n < 32 + SUBS))
         def _():
             iota_u = lax.broadcasted_iota(jnp.int32, (BLK, 128), 0) + (n - 32) * BLK
             onehot_a[n - 32] = (iota_u == ids_a).astype(BF16)
 
-        @when_at(n, 45)
+        @when_at(n, 43)
         def _():
             last_item = item_sum(2)
             tot = (ei_all[0, r].astype(F32) + ei_all[1, r].astype(F32) + ei_all[2, r].astype(F32)
                    + last_item.astype(F32))
             out_item = (tot / (LAYERS + 1)).astype(BF16)
             outi[...] = out_item
+            item_out.start()
             item_share(2, out_item)
 
-        @when_at(n, 46)
+        @when_at(n, 44)
         def _():
             item_end(2)
             iota_i = lax.broadcasted_iota(jnp.int32, (BLK, 128), 0) + c * BLK
@@ -531,7 +549,7 @@
             col_send(2 * SUBS, lambda cc: pk.at[r], pk_recv.at[c])
             pk_recv[c] = pk[r]
 
-        @when_at(n, 44)
+        @when_at(n, 42)
         def _():
             item_start(2)
         return carry
@@ -554,6 +572,9 @@
         remote(ref, ref, sem, y_rs.at[0], mate).wait_send()
 
     drain(ysend, y_ss)
+    for q in range(SUBS):
+        table_out(q).wait()
+    item_out.wait()
     drain(yrecv.at[:, pl.ds(0, DEPTH - 1)], z_ss)
     drain(panels.at[:, pl.ds(0, 1)], ag_sy)
     for at in range(DEPTH):
@@ -581,18 +602,23 @@
 def solution(mesh):
     def local_prog(mask_blk, user_shard, item_shard, triples):
         vmem = pl.BlockSpec(memory_space=pltpu.VMEM)
+        hbm = pl.BlockSpec(memory_space=pl.ANY)
         dma = pltpu.SemaphoreType.DMA
         outu, outi, loss = pl.pallas_call(
             kernel,
             out_shape=(jax.ShapeDtypeStruct((SUBS, DIM, BLK), BF16),
                        jax.ShapeDtypeStruct((DIM, 128), BF16),
                        jax.ShapeDtypeStruct((8, 128), F32)),
-            in_specs=[pl.BlockSpec(memory_space=pl.ANY), vmem, vmem, vmem],
-            out_specs=(vmem, vmem, vmem),
+            in_specs=[hbm] * 4,
+            out_specs=(hbm, hbm, vmem),
             scratch_shapes=[
                 pltpu.VMEM((RING * SUBS, BLK, BLK), BF16),
                 pltpu.VMEM((MASK_BUFS, BLK, BLK), jnp.int32),
                 dma((MASK_BUFS,)),
+                dma((SUBS + 2,)),
+                pltpu.VMEM((3, 128), jnp.int32),
+                pltpu.VMEM((SUBS, DIM, BLK), BF16),
+                pltpu.VMEM((DIM, 128), BF16),
                 pltpu.VMEM((LAYERS, RING, SUBS, DIM, BLK), BF16),
                 pltpu.VMEM((LAYERS + 1, ROWS, DIM, 128), BF16),
                 pltpu.VMEM((LAYERS, DIM, BLK), F32),

time: 186 us -> 182 us (0.978)
  Pallas kernels: 185 us -> 181 us
    pallas_call x1, Pallas kernels: 184 us -> 179 us  [local_prog(): pl.pallas_call(kernel, out_shape=(jax.ShapeDtypeStruct((SUBS, DIM, BLK),...]
where the time goes in v5:
time: 182 us
  Pallas kernels  181 us (99%)
    pallas_call x1, Pallas kernels, local_prog(): pl.pallas_call(kernel, out_shape=(jax.ShapeDtypeStruct((SUBS, DIM, BLK),...  179 us

profile of v5, /device:TPU:0, one launch (start us, length us, event | category | flops | bytes accessed | tf_op | source)
XLA Modules:
  0.0 181.7 jit_solution(18265991637891362954)
XLA Ops:
  0.6 179.4 %propagate.1 = (bf16[4,64,512]{2,1,0:T(8,128)(2,1)}, bf16[64,128]{1,0:T(8,128)(2,1)}, f32[8,128]{1,0:T(8,128)}) custom-call(s32[16384,512]{1,0:T(8,128)} %mask_hbm.1, bf16[64,2048]{1,0:T(8,128)(2,1)} %bitcast.6, bf16[64,128]{1,0:T(8,128)(2,1)} %bitcast.7, s32[3,128]{1,0:T(4,128)} %bitcast.8), custom_call_target="tpu_custom_call" | custom-call | tf_op jit(solution)/shard_map/propagate/pallas_call | solution.py:607
  180.0 1.7 deliver.1

commit v6 on v5

--- a/solution.py
+++ b/solution.py
@@ -34,7 +34,7 @@
            panels, ei_all, item_acc, item_send, item_recv,
            ysend, yrecv, zin,
            colsum, deg_part, deg_recv, scale_u, itemdeg, itemdeg_recv, scale_v,
-           onehot_a, pk, pk_recv, picks, user_vec, terms, terms2,
+           onehot_a, pk, pk_recv, picks, user_vec, terms, term_sem,
            y_ss, y_rs, z_ss, z_rs, ag_sy, ag_su, ag_sd, ag_rs,
            row_ss, row_rs, col_ss, col_rs):
     c = lax.axis_index("col")
@@ -67,10 +67,10 @@
     trip_in.start()
 
     barrier = pltpu.get_barrier_semaphore()
-    for rr in row_peers:
-        pl.semaphore_signal(barrier, inc=1, device_id=(c, rr), device_id_type=MESH)
-    for cc in col_peers:
-        pl.semaphore_signal(barrier, inc=1, device_id=(cc, r), device_id_type=MESH)
+    all_peers = [(lax.rem(c + dc, RING), lax.rem(r + dr, ROWS))
+                 for dc in range(RING) for dr in range(ROWS) if dc or dr]
+    for peer in all_peers:
+        pl.semaphore_signal(barrier, inc=1, device_id=peer, device_id_type=MESH)
 
     def remote(src, dst, ss, rs, col):
         return pltpu.make_async_remote_copy(src_ref=src, dst_ref=dst, send_sem=ss, recv_sem=rs,
@@ -209,7 +209,7 @@
     item_in.wait()
     trip_in.wait()
     with jax.named_scope("entry"):
-        pl.semaphore_wait(barrier, (ROWS - 1) + (RING - 1))
+        pl.semaphore_wait(barrier, len(all_peers))
     deg_send(0)
     ag_own(0, 0)
     ag_own(0, 1)
@@ -562,11 +562,11 @@
               - jnp.sum(ea * both[:, 128:256], axis=0, keepdims=True))
     term = jnp.maximum(-margin, 0.0) + jnp.log1p(jnp.exp(-jnp.abs(margin)))
     mine = jnp.logical_and(ids_a >= 0, ids_a < SUBS * BLK)
-    terms[r] = jnp.where(mine, term, 0.0)
-    row_send(9, lambda rr: terms.at[r], terms.at[r])
-    row_wait(9, terms.at[pl.ds(0, ROWS - 1)])
-    terms2[c] = terms[0] + terms[1] + terms[2] + terms[3]
-    col_send(2 * SUBS + 1, lambda cc: terms2.at[c], terms2.at[c])
+    me = c * ROWS + r
+    terms[me] = jnp.where(mine, term, 0.0)
+    for peer in all_peers:
+        pltpu.make_async_remote_copy(src_ref=terms.at[me], dst_ref=terms.at[me], send_sem=term_sem.at[0],
+                                     recv_sem=term_sem.at[1], device_id=peer, device_id_type=MESH).start()
 
     def drain(ref, sem):
         remote(ref, ref, sem, y_rs.at[0], mate).wait_send()
@@ -585,10 +585,15 @@
             if at > 0:
                 drain(panels.at[:, pl.ds(0, 2 * (DEPTH - at))], ag_sd)
 
-    col_wait(2 * SUBS + 1, terms2.at[pl.ds(0, RING - 1)])
-    tsum = terms2[0]
-    for q in range(1, RING):
-        tsum = tsum + terms2[q]
+    with jax.named_scope("terms_wait"):
+        rest = terms.at[pl.ds(0, len(all_peers))]
+        cp = pltpu.make_async_remote_copy(src_ref=rest, dst_ref=rest, send_sem=term_sem.at[0],
+                                          recv_sem=term_sem.at[1], device_id=all_peers[0], device_id_type=MESH)
+        cp.wait_recv()
+        cp.wait_send()
+    tsum = terms[0]
+    for q in range(1, RING * ROWS):
+        tsum = tsum + terms[q]
     loss[...] = jnp.broadcast_to(jnp.sum(tsum, axis=1, keepdims=True) / tsum.shape[1], loss.shape)
 
 
@@ -639,11 +644,11 @@
                 pltpu.VMEM((RING, 16, 256), BF16),
                 pltpu.VMEM((ROWS, 16, 256), BF16),
                 pltpu.VMEM((DIM, 128), F32),
-                pltpu.VMEM((ROWS, 1, 128), F32),
-                pltpu.VMEM((RING, 1, 128), F32),
+                pltpu.VMEM((RING * ROWS, 1, 128), F32),
+                dma((2,)),
                 dma, dma((Y_SEMS,)), dma, dma((DEPTH + 1, SUBS)),
                 dma, dma, dma, dma((2, RING, SUBS)),
-                dma((10,)), dma((10,)), dma((2 * SUBS + 2,)), dma((2 * SUBS + 2,)),
+                dma((9,)), dma((9,)), dma((2 * SUBS + 1,)), dma((2 * SUBS + 1,)),
             ],
             compiler_params=pltpu.CompilerParams(
                 collective_id=0, has_side_effects=True, vmem_limit_bytes=61 * 1024 * 1024),

time: 182 us -> 180 us (0.989)
  Pallas kernels: 181 us -> 179 us
    pallas_call x1, Pallas kernels: 179 us -> 177 us  [local_prog(): pl.pallas_call(kernel, out_shape=(jax.ShapeDtypeStruct((SUBS, DIM, BLK),...]
where the time goes in v6:
time: 180 us
  Pallas kernels  179 us (99%)
    pallas_call x1, Pallas kernels, local_prog(): pl.pallas_call(kernel, out_shape=(jax.ShapeDtypeStruct((SUBS, DIM, BLK),...  177 us

profile of v6, /device:TPU:0, one launch (start us, length us, event | category | flops | bytes accessed | tf_op | source)
XLA Modules:
  0.0 179.6 jit_solution(8549025499221887435)
XLA Ops:
  0.6 177.2 %propagate.1 = (bf16[4,64,512]{2,1,0:T(8,128)(2,1)}, bf16[64,128]{1,0:T(8,128)(2,1)}, f32[8,128]{1,0:T(8,128)}) custom-call(s32[16384,512]{1,0:T(8,128)} %mask_hbm.1, bf16[64,2048]{1,0:T(8,128)(2,1)} %bitcast.6, bf16[64,128]{1,0:T(8,128)(2,1)} %bitcast.7, s32[3,128]{1,0:T(4,128)} %bitcast.8), custom_call_target="tpu_custom_call" | custom-call | tf_op jit(solution)/shard_map/propagate/pallas_call | solution.py:612
  177.9 1.7 deliver.1

commit v7 on v6

--- a/solution.py
+++ b/solution.py
@@ -10,8 +10,11 @@
 ROWS = 4
 DEPTH = 4
 ROUNDS = 16
-AHEAD = 2
+AHEAD = 3
 Y_SEMS = 8
+X_LO = 2
+X_HI = 3
+X_LEAD = 2
 SUBS = 4
 DIM = 64
 BLK = 512
@@ -32,10 +35,10 @@
 def kernel(mask_hbm, euT, eiT, trip_hbm, outu_hbm, outi_hbm, loss,
            adj, mbuf, msem, io_sem, trip, outu, outi,
            panels, ei_all, item_acc, item_send, item_recv,
-           ysend, yrecv, zin,
+           ysend, yrecv, zin, xin,
            colsum, deg_part, deg_recv, scale_u, itemdeg, itemdeg_recv, scale_v,
            onehot_a, pk, pk_recv, picks, user_vec, terms, term_sem,
-           y_ss, y_rs, z_ss, z_rs, ag_sy, ag_su, ag_sd, ag_rs,
+           y_ss, y_rs, x_ss, x_rs, z_ss, z_rs, ag_sy, ag_su, ag_sd, ag_rs,
            row_ss, row_rs, col_ss, col_rs):
     c = lax.axis_index("col")
     r = lax.axis_index("row")
@@ -279,14 +282,47 @@
         pw = 1 + 3 * g + 9 * lax.div(g * (g - 1), 2) + 27 * lax.div(g * (g - 1) * (g - 2), 6)
         return k, lax.rem(lax.div(27 + 48 * z + 57 * lax.div(z, 2), pw), DEPTH), q
 
+    def y_set(k, q):
+        later = lax.div(k + 1, 2)
+        skip = lax.div(q + SUBS - X_LO, SUBS) * (1 - lax.div(q + SUBS - X_HI, SUBS))
+        return later + (1 - later) * 2 * skip
+
     def y_copy(n):
         k, t, q = place(n)
-        return remote(ysend.at[k, t, q], yrecv.at[k, t, q], y_ss, y_rs.at[lax.rem(n, Y_SEMS)], mate)
+        return remote(ysend.at[k, t, q], yrecv.at[k, t, q], y_ss.at[y_set(k, q)], y_rs.at[lax.rem(n, Y_SEMS)], mate)
+
+    def is_middle(s):
+        return lax.div(s * (DEPTH - 1 - s), 2)
+
+    inner = 1 + lax.rem(z, 2)
+    x_from = lax.div(z, 2)
+    x_last = 2 - is_middle(z)
+
+    def skips_y(n):
+        return jnp.logical_and(lax.rem(n, DEPTH) == x_last, jnp.logical_and(n >= 4 * X_LO, n < 4 * X_HI))
+
+    def x_copy(q, side):
+        return remote(ysend.at[0, inner, q], xin.at[side, q], x_ss.at[q], x_rs.at[side, q], 2 * inner + y)
+
+    def x_begin(q):
+        ysend[0, inner, q] = user_part(0, (2 * inner + 1 - y) * SUBS + q)
+        x_copy(q, x_from).start()
 
     def y_begin(n):
         k, t, q = place(n)
-        ysend[k, t, q] = user_part(k, (2 * t + 1 - y) * SUBS + q)
-        y_copy(n).start()
+
+        @pl.when(jnp.logical_not(skips_y(n)))
+        def _():
+            ysend[k, t, q] = user_part(k, (2 * t + 1 - y) * SUBS + q)
+            takes = jnp.logical_and(lax.rem(n, DEPTH) == DEPTH - 1, jnp.logical_and(n >= 4 * X_LO, n < 4 * X_HI))
+
+            @pl.when(jnp.logical_and(is_mid, takes))
+            def _():
+                for side in range(2):
+                    with jax.named_scope("rs_x"):
+                        x_copy(q, side).wait_recv()
+                    ysend[k, t, q] = ysend[k, t, q] + xin[side, q]
+            y_copy(n).start()
 
     def z_up(k, t, q):
         return remote(yrecv.at[k, t, q], zin.at[k, t, q], z_ss, z_rs.at[t, q], c + 2)
@@ -312,9 +348,17 @@
     def y_stage(n):
         k, t, q = place(n)
         part = user_part(k, (2 * t + y) * SUBS + q)
-        with jax.named_scope("rs_y"):
-            y_copy(n).wait_recv()
-        yrecv[k, t, q] = yrecv[k, t, q] + part
+        skipped = skips_y(n)
+
+        @pl.when(skipped)
+        def _():
+            yrecv[k, t, q] = part
+
+        @pl.when(jnp.logical_not(skipped))
+        def _():
+            with jax.named_scope("rs_y"):
+                y_copy(n).wait_recv()
+            yrecv[k, t, q] = yrecv[k, t, q] + part
 
         @pl.when(jnp.logical_and(jnp.logical_not(is_mid), t != z))
         def _():
@@ -369,9 +413,6 @@
     ids_a = trip[0:1, :] - base
     item_acc[...] = jnp.zeros_like(item_acc)
     user_vec[...] = jnp.zeros_like(user_vec)
-
-    def is_middle(s):
-        return lax.div(s * (DEPTH - 1 - s), 2)
 
     own_lag = 7 - 2 * is_middle(z)
     sets = SUBS * (LAYERS - 1)
@@ -414,14 +455,13 @@
     def one_round(n, carry):
         @when_at(n, 1)
         def _():
-            deg_end(1)
             deg_sum(3)
 
-        @when_at(n, 3)
+        @when_at(n, 2)
         def _():
             deg_end(2)
 
-        @when_at(n, 5)
+        @when_at(n, 4)
         def _():
             deg_end(3)
 
@@ -433,6 +473,10 @@
         def _():
             y_begin(n + AHEAD)
 
+        @pl.when(jnp.logical_and(lax.rem(n + X_LEAD, DEPTH) == 0,
+                                 jnp.logical_and(n + X_LEAD >= 4 * X_LO, n + X_LEAD < 4 * X_HI)))
+        def _():
+            x_begin(lax.div(n + X_LEAD, DEPTH))
         gather_mate(2 * n)
         for d, f in ((1, 0), (2, 1), (3, 0)):
             gather_line(2 * n, d, f)
@@ -462,10 +506,14 @@
         def _():
             own_stage(n)
 
-        @pl.when(jnp.logical_and(n >= 1, n < 7))
-        def _():
-            build_round(2 * n + 2)
-            build_round(2 * n + 3)
+        @when_at(n, 0)
+        def _():
+            deg_end(1)
+
+        @pl.when(n < 6)
+        def _():
+            build_round(2 * n + 4)
+            build_round(2 * n + 5)
 
         @pl.when(n < 6)
         def _():
@@ -518,7 +566,7 @@
         def _():
             item_share(1, item_sum(1))
 
-        @when_at(n, 29)
+        @when_at(n, 28)
         def _():
             item_end(1)
 
@@ -571,7 +619,11 @@
     def drain(ref, sem):
         remote(ref, ref, sem, y_rs.at[0], mate).wait_send()
 
-    drain(ysend, y_ss)
+    drain(ysend.at[pl.ds(1, LAYERS - 1)], y_ss.at[1])
+    drain(ysend.at[0, :, pl.ds(0, SUBS - X_HI + X_LO)], y_ss.at[0])
+    drain(ysend.at[0, pl.ds(0, DEPTH - 1), pl.ds(0, X_HI - X_LO)], y_ss.at[2])
+    for q in range(X_LO, X_HI):
+        drain(xin.at[0, q], x_ss.at[q])
     for q in range(SUBS):
         table_out(q).wait()
     item_out.wait()
@@ -632,6 +684,7 @@
                 pltpu.VMEM((LAYERS, DEPTH, SUBS, DIM, BLK), F32),
                 pltpu.VMEM((LAYERS, DEPTH, SUBS, DIM, BLK), F32),
                 pltpu.VMEM((LAYERS, DEPTH + 1, SUBS, DIM, BLK), F32),
+                pltpu.VMEM((2, SUBS, DIM, BLK), F32),
                 pltpu.VMEM((8, BLK), F32),
                 pltpu.VMEM((RING * SUBS, 1, BLK), F32),
                 pltpu.VMEM((RING, SUBS, 1, BLK), F32),
@@ -646,7 +699,7 @@
                 pltpu.VMEM((DIM, 128), F32),
                 pltpu.VMEM((RING * ROWS, 1, 128), F32),
                 dma((2,)),
-                dma, dma((Y_SEMS,)), dma, dma((DEPTH + 1, SUBS)),
+                dma((3,)), dma((Y_SEMS,)), dma((SUBS,)), dma((2, SUBS)), dma, dma((DEPTH + 1, SUBS)),
                 dma, dma, dma, dma((2, RING, SUBS)),
                 dma((9,)), dma((9,)), dma((2 * SUBS + 1,)), dma((2 * SUBS + 1,)),
             ],

time: 180 us -> 177 us (0.983)
  Pallas kernels: 179 us -> 176 us
    pallas_call x1, Pallas kernels: 177 us -> 175 us  [local_prog(): pl.pallas_call(kernel, out_shape=(jax.ShapeDtypeStruct((SUBS, DIM, BLK),...]
where the time goes in v7:
time: 177 us
  Pallas kernels  176 us (99%)
    pallas_call x1, Pallas kernels, local_prog(): pl.pallas_call(kernel, out_shape=(jax.ShapeDtypeStruct((SUBS, DIM, BLK),...  175 us

profile of v7, /device:TPU:0, one launch (start us, length us, event | category | flops | bytes accessed | tf_op | source)
XLA Modules:
  0.0 177.1 jit_solution(1763139541629427785)
XLA Ops:
  0.6 174.7 %propagate.1 = (bf16[4,64,512]{2,1,0:T(8,128)(2,1)}, bf16[64,128]{1,0:T(8,128)(2,1)}, f32[8,128]{1,0:T(8,128)}) custom-call(s32[16384,512]{1,0:T(8,128)} %mask_hbm.1, bf16[64,2048]{1,0:T(8,128)(2,1)} %bitcast.6, bf16[64,128]{1,0:T(8,128)(2,1)} %bitcast.7, s32[3,128]{1,0:T(4,128)} %bitcast.8), custom_call_target="tpu_custom_call" | custom-call | tf_op jit(solution)/shard_map/propagate/pallas_call | solution.py:664
  175.4 1.7 deliver.1

commit v8 on v7

--- a/solution.py
+++ b/solution.py
@@ -12,6 +12,7 @@
 ROUNDS = 16
 AHEAD = 3
 Y_SEMS = 8
+ROW_SET = (0, 1, 2, 1, 2, 1, 2, 1, 2)
 X_LO = 2
 X_HI = 3
 X_LEAD = 2
@@ -145,12 +146,12 @@
 
     def row_send(u, src, dst):
         for rr in row_peers:
-            pltpu.make_async_remote_copy(src_ref=src(rr), dst_ref=dst, send_sem=row_ss.at[u], recv_sem=row_rs.at[u],
+            pltpu.make_async_remote_copy(src_ref=src(rr), dst_ref=dst, send_sem=row_ss.at[ROW_SET[u]], recv_sem=row_rs.at[ROW_SET[u]],
                                          device_id=(c, rr), device_id_type=MESH).start()
 
     def row_wait(u, ref):
         with jax.named_scope("row_wait_%d" % u):
-            cp = pltpu.make_async_remote_copy(src_ref=ref, dst_ref=ref, send_sem=row_ss.at[u], recv_sem=row_rs.at[u],
+            cp = pltpu.make_async_remote_copy(src_ref=ref, dst_ref=ref, send_sem=row_ss.at[ROW_SET[u]], recv_sem=row_rs.at[ROW_SET[u]],
                                               device_id=(c, row_peers[0]), device_id_type=MESH)
             cp.wait_recv()
             cp.wait_send()
@@ -222,8 +223,8 @@
     ag_own(0, 2)
     mask_quarter(2)
     deg_send(2)
+    deg_sum(0)
     ag_own(0, 3)
-    deg_sum(0)
     for q in range(2):
         ag_mate(0, q)
         early_event(q)
@@ -701,7 +702,7 @@
                 dma((2,)),
                 dma((3,)), dma((Y_SEMS,)), dma((SUBS,)), dma((2, SUBS)), dma, dma((DEPTH + 1, SUBS)),
                 dma, dma, dma, dma((2, RING, SUBS)),
-                dma((9,)), dma((9,)), dma((2 * SUBS + 1,)), dma((2 * SUBS + 1,)),
+                dma((3,)), dma((3,)), dma((2 * SUBS + 1,)), dma((2 * SUBS + 1,)),
             ],
             compiler_params=pltpu.CompilerParams(
                 collective_id=0, has_side_effects=True, vmem_limit_bytes=61 * 1024 * 1024),

time: 177 us -> 177 us (level)
  no operation moved by 1% of the time
where the time goes in v8:
time: 177 us
  Pallas kernels  176 us (99%)
    pallas_call x1, Pallas kernels, local_prog(): pl.pallas_call(kernel, out_shape=(jax.ShapeDtypeStruct((SUBS, DIM, BLK),...  175 us

profile of v8, /device:TPU:0, one launch (start us, length us, event | category | flops | bytes accessed | tf_op | source)
XLA Modules:
  0.0 176.9 jit_solution(10454993794854991319)
XLA Ops:
  0.6 174.6 %propagate.1 = (bf16[4,64,512]{2,1,0:T(8,128)(2,1)}, bf16[64,128]{1,0:T(8,128)(2,1)}, f32[8,128]{1,0:T(8,128)}) custom-call(s32[16384,512]{1,0:T(8,128)} %mask_hbm.1, bf16[64,2048]{1,0:T(8,128)(2,1)} %bitcast.6, bf16[64,128]{1,0:T(8,128)(2,1)} %bitcast.7, s32[3,128]{1,0:T(4,128)} %bitcast.8), custom_call_target="tpu_custom_call" | custom-call | tf_op jit(solution)/shard_map/propagate/pallas_call | solution.py:665
  175.2 1.7 deliver.1

commit v9 on v8

--- a/solution.py
+++ b/solution.py
@@ -81,7 +81,7 @@
                                             device_id=(col, r), device_id_type=MESH)
 
     def ag_rs_of(k, col, q):
-        return ag_rs.at[lax.div(k + 1, 2), col, q]
+        return ag_rs.at[col, q]
 
     def ag_y(k, q, col):
         ref = panels.at[k, col, q]
@@ -701,7 +701,7 @@
                 pltpu.VMEM((RING * ROWS, 1, 128), F32),
                 dma((2,)),
                 dma((3,)), dma((Y_SEMS,)), dma((SUBS,)), dma((2, SUBS)), dma, dma((DEPTH + 1, SUBS)),
-                dma, dma, dma, dma((2, RING, SUBS)),
+                dma, dma, dma, dma((RING, SUBS)),
                 dma((3,)), dma((3,)), dma((2 * SUBS + 1,)), dma((2 * SUBS + 1,)),
             ],
             compiler_params=pltpu.CompilerParams(

time: 177 us -> 177 us (level)
  no operation moved by 1% of the time
where the time goes in v9:
time: 177 us
  Pallas kernels  176 us (99%)
    pallas_call x1, Pallas kernels, local_prog(): pl.pallas_call(kernel, out_shape=(jax.ShapeDtypeStruct((SUBS, DIM, BLK),...  174 us

profile of v9, /device:TPU:0, one launch (start us, length us, event | category | flops | bytes accessed | tf_op | source)
XLA Modules:
  0.0 176.6 jit_solution(12756524706427519111)
XLA Ops:
  0.6 174.3 %propagate.1 = (bf16[4,64,512]{2,1,0:T(8,128)(2,1)}, bf16[64,128]{1,0:T(8,128)(2,1)}, f32[8,128]{1,0:T(8,128)}) custom-call(s32[16384,512]{1,0:T(8,128)} %mask_hbm.1, bf16[64,2048]{1,0:T(8,128)(2,1)} %bitcast.6, bf16[64,128]{1,0:T(8,128)(2,1)} %bitcast.7, s32[3,128]{1,0:T(4,128)} %bitcast.8), custom_call_target="tpu_custom_call" | custom-call | tf_op jit(solution)/shard_map/propagate/pallas_call | solution.py:665
  174.9 1.7 deliver.1
